TPU v7x, 256 devices: a whole 4x4x8 slice. The times are simulated.
256 devices in a mesh: section: 32 (over x, z_hi, core), dp: 8 (over z_lo, y).
Axes of the slice: x: 4, y: 4, z: 8 (z_hi: 4, z_lo: 2; z = z_hi * 2 + z_lo), core: 2. Of those that a mesh axis runs over, the one named last changes fastest.
Arguments:
- w_value: bfloat16 [32, 2, 4608, 1024], P('section', None, None, 'dp'), may hold values from -0.09375 to 0.09375
- w_out: bfloat16 [32, 2, 1024, 4608], P('section', None, 'dp'), may hold values from -0.1875 to 0.1875
- norm_gain: float32 [32, 2, 4608], P('section'), may hold values from 0.5 to 1.5
- saved_inputs: bfloat16 [32, 3, 2, 64, 4608], P('section', None, None, 'dp'), may hold values from -6 to 6
- arriving: bfloat16 [32, 2, 64, 4608], P('section', None, 'dp'), may hold values from -6 to 6
- returning: bfloat16 [32, 2, 64, 4608], P('section', None, 'dp'), may hold values from -6 to 6
- fresh_rows: bfloat16 [4, 64, 4608], P(None, 'dp'), may hold values from -6 to 6
- targets: bfloat16 [4, 64, 4608], P(None, 'dp'), may hold values from -6 to 6
- fill_slots: int32 [32, 4, 2], P('section'), may hold values from 0 to 2
- read_slots: int32 [32, 4, 2], P('section'), may hold values from 0 to 2
Outputs:
- activ_out: bfloat16 [32, 2, 64, 4608], P('section', None, 'dp')
- cotan_out: bfloat16 [32, 2, 64, 4608], P('section', None, 'dp')
- stash_out: bfloat16 [32, 3, 2, 64, 4608], P('section', None, None, 'dp')
- grad_value: bfloat16 [32, 2, 4608, 1024], P('section', None, None, 'dp')
- grad_out: bfloat16 [32, 2, 1024, 4608], P('section', None, 'dp')
- grad_gain: float32 [32, 2, 4608], P('section')
All inputs are finite; a program needn't handle non-finite values.
Results may differ from a plain program's by a relative error of at most 0.029.
Values may be sent and summed in bfloat16 or wider, within the bound.
A program may use at most 128 MiB of HBM per device.

v0:
```python
import jax
import jax.numpy as jnp
from jax import lax
from jax.sharding import PartitionSpec as P

epsilon = 1e-06


def in_order(tiles, dim):
    tiles = jnp.moveaxis(tiles, 0, dim)
    lengths = tiles.shape
    return tiles.reshape(*lengths[:dim], lengths[dim] * lengths[dim + 1], *lengths[dim + 2 :])


def copy_for_each(shard, axis):
    copies = jnp.broadcast_to(shard, (lax.axis_size(axis), *shard.shape))
    return lax.all_to_all(copies, axis, split_axis=0, concat_axis=0, tiled=True)


def collect(shard, axis, dim):
    return in_order(copy_for_each(shard, axis), dim)


def in_blocks(shard, dim, devices):
    before, after = (shard.shape[:dim], shard.shape[dim + 1 :])
    return jnp.moveaxis(shard.reshape(*before, devices, -1, *after), dim, 0)


def sum_at_owner(shard, axis, dim):
    tiles = in_blocks(shard, dim, lax.axis_size(axis))
    arrived = lax.all_to_all(tiles, axis, split_axis=0, concat_axis=0, tiled=True)
    return arrived.astype(jnp.float32).sum(axis=0)


def shifted(shard, axis, by):
    devices = lax.axis_size(axis)
    return lax.ppermute(shard, axis, [(i, (i + by) % devices) for i in range(devices)])


def side_by_side(arrays, axis, dim, along):
    ends, at = ([], 0)
    for a in arrays[:-1]:
        at += a.shape[along]
        ends.append(at)
    both = jnp.concatenate(arrays, axis=along)
    return tuple(jnp.split(collect(both, axis, dim), ends, axis=along))


def taken_together(shard, axis):
    return copy_for_each(shard, axis).astype(jnp.float32).sum(axis=0)


def normalize(block_rows, gain_row):
    values = block_rows.astype(jnp.float32)
    inv_root = lax.rsqrt(jnp.mean(values * values, axis=-1, keepdims=True) + epsilon)
    scaled = values * inv_root
    return (scaled, inv_root, (scaled * gain_row).astype(jnp.bfloat16))


def times_transposed(left, right):
    return lax.dot_general(
        left, right, (((1,), (1,)), ((), ())), preferred_element_type=jnp.float32
    )


def transposed_times(left, right):
    return lax.dot_general(
        left, right, (((0,), (0,)), ((), ())), preferred_element_type=jnp.float32
    )


def weight_terms(value_group, normed_all, down_grad, upstream_all):
    values = jnp.dot(normed_all, value_group, preferred_element_type=jnp.float32).astype(
        jnp.bfloat16
    )
    return (transposed_times(normed_all, down_grad), transposed_times(values, upstream_all))


def body(
    w_value,
    w_out,
    norm_gain,
    saved_inputs,
    arriving,
    returning,
    fresh_rows,
    targets,
    fill_slots,
    read_slots,
):
    value_mats = w_value[0]
    out_mats = w_out[0]
    gains = norm_gain[0]
    saved = saved_inputs[0]
    activations = arriving[0]
    cotangents = returning[0]
    tick_count = fresh_rows.shape[0]
    tok_rows = activations.shape[1]
    all_rows = tok_rows * lax.axis_size("dp")
    section_index = lax.axis_index("section")
    last_section = lax.axis_size("section") - 1

    def forward(block, group):
        scaled, inv_root, normed = normalize(block, gains[group])
        values = jnp.dot(
            collect(normed, "dp", 0), value_mats[group], preferred_element_type=jnp.float32
        ).astype(jnp.bfloat16)
        summed = sum_at_owner(
            jnp.dot(values, out_mats[group], preferred_element_type=jnp.float32).astype(
                jnp.bfloat16
            ),
            "dp",
            0,
        )
        return (block.astype(jnp.float32) + summed).astype(jnp.bfloat16)

    value_sums = [jnp.zeros(value_mats.shape[1:], jnp.float32) for group in range(2)]
    out_sums = [jnp.zeros(out_mats.shape[1:], jnp.float32) for group in range(2)]
    gain_sums = [jnp.zeros(gains.shape[1:], jnp.float32) for group in range(2)]
    outputs = activations
    gradients = cotangents
    for tick_index in range(tick_count):
        if tick_index > 0:
            received = shifted(outputs, "section", 1)
            lower_group = jnp.where(section_index == 0, fresh_rows[tick_index], received[0])
            upper_group = jnp.where(section_index == 0, received[0], received[1])
            activations = jnp.stack([lower_group, upper_group])
            returned = shifted(gradients, "section", -1)
            finish = (
                outputs[1].astype(jnp.float32) - targets[tick_index - 1].astype(jnp.float32)
            ).astype(jnp.bfloat16)
            cotangents = jnp.stack(
                [
                    jnp.where(section_index == last_section, returned[1], returned[0]),
                    jnp.where(section_index == last_section, finish, returned[1]),
                ]
            )
        for group in range(2):
            saved = saved.at[fill_slots[0, tick_index, group], group].set(activations[group])
        outputs = jnp.stack([forward(activations[0], 0), forward(activations[1], 1)])
        fresh_grads = []
        for group in range(2):
            source = saved[read_slots[0, tick_index, group], group]
            scaled, inv_root, normed = normalize(source, gains[group])
            normed_all, upstream_all = side_by_side((normed, cotangents[group]), "dp", 0, 1)
            down_grad = times_transposed(upstream_all, out_mats[group]).astype(jnp.bfloat16)
            pulled = sum_at_owner(
                times_transposed(down_grad, value_mats[group]).astype(jnp.bfloat16), "dp", 0
            )
            weighted = pulled * gains[group]
            inner_mean = jnp.mean(weighted * scaled, axis=-1, keepdims=True)
            fresh_grads.append(
                (
                    cotangents[group].astype(jnp.float32)
                    + inv_root * (weighted - scaled * inner_mean)
                ).astype(jnp.bfloat16)
            )
            gain_sums[group] = gain_sums[group] + jnp.sum(pulled * scaled, axis=0)
            value_term, out_term = weight_terms(
                value_mats[group], normed_all, down_grad, upstream_all
            )
            value_sums[group] = value_sums[group] + value_term
            out_sums[group] = out_sums[group] + out_term
        gradients = jnp.stack(fresh_grads)
    grad_scale = (tick_count * all_rows) ** (-0.5)
    gain_total = taken_together(jnp.stack(gain_sums).astype(jnp.bfloat16), "dp").astype(jnp.float32)
    final_rows = jnp.stack([outputs[0], outputs[1]])
    return (
        final_rows[None],
        gradients[None],
        saved[None],
        (jnp.stack(value_sums) * grad_scale).astype(jnp.bfloat16)[None],
        (jnp.stack(out_sums) * grad_scale).astype(jnp.bfloat16)[None],
        (gain_total * grad_scale)[None],
    )


def solution(mesh):
    in_specs = (
        P("section", None, None, "dp"),
        P("section", None, "dp", None),
        P("section", None, None),
        P("section", None, None, "dp", None),
        P("section", None, "dp", None),
        P("section", None, "dp", None),
        P(None, "dp", None),
        P(None, "dp", None),
        P("section", None, None),
        P("section", None, None),
    )
    out_specs = (
        P("section", None, "dp", None),
        P("section", None, "dp", None),
        P("section", None, None, "dp", None),
        P("section", None, None, "dp"),
        P("section", None, "dp", None),
        P("section", None, None),
    )
    return jax.shard_map(body, mesh=mesh, in_specs=in_specs, out_specs=out_specs, check_vma=False)
```

profile of v0, /device:TPU:32, one launch (start us, length us, event | category | flops | bytes accessed | tf_op | source)
XLA Modules:
  0.0 627.9 jit_solution(8871406859827024366)
XLA Ops:
  19.3 5.9 all-to-all-start.18
  25.2 15.6 %all-to-all-done.18 = bf16[8,8,9216]{2,1,0:T(8,128)(2,1)S(1)} async-done(((bf16[8,8,9216]{2,1,0:T(8,128)(2,1)}), bf16[8,8,9216]{2,1,0:T(8,128)(2,1)S(1)}, u32[]{:S(2)}, u32[]{:S(2)}) %all-to-all-start.18) | async-done | bytes 1179680 | tf_op jit(solution)/shard_map/all_to_all | solution.py:17
  51.7 12.0 %all-to-all-done.16 = bf16[8,8,9216]{2,1,0:T(8,128)(2,1)} async-done(((bf16[8,8,9216]{2,1,0:T(8,128)(2,1)}), bf16[8,8,9216]{2,1,0:T(8,128)(2,1)}, u32[]{:S(2)}, u32[]{:S(2)}) %all-to-all-start.16) | async-done | bytes 1179680 | tf_op jit(solution)/shard_map/all_to_all | solution.py:17
  84.2 7.6 %all-to-all-done.17 = bf16[8,8,4608]{2,1,0:T(8,128)(2,1)} async-done(((bf16[8,8,4608]{2,1,0:T(8,128)(2,1)}), bf16[8,8,4608]{2,1,0:T(8,128)(2,1)}, u32[]{:S(2)}, u32[]{:S(2)}) %all-to-all-start.17) | async-done | bytes 589856 | tf_op jit(solution)/shard_map/all_to_all | solution.py:31
  93.3 13.6 %all_to_all.165 = bf16[8,8,4608]{2,1,0:T(8,128)(2,1)} all-to-all(bf16[8,8,4608]{2,1,0:T(8,128)(2,1)S(1)} %broadcast_in_dim.111), channel_id=1, replica_groups=mesh['section'=32,'dp'=8] {'dp'}, dimensions={0} | all-to-all | bytes 1179648 | tf_op jit(solution)/shard_map/all_to_all | solution.py:17
  151.6 8.7 %collective-permute-done = bf16[2,8,4608]{2,1,0:T(8,128)(2,1)S(1)} collective-permute-done((bf16[2,8,4608]{2,1,0:T(8,128)(2,1)S(1)}, bf16[2,8,4608]{2,1,0:T(8,128)(2,1)S(1)}, u32[]{:S(2)}, u32[]{:S(2)}) %collective-permute-start) | collective-permute-done | bytes 147488 | tf_op jit(solution)/shard_map/ppermute | solution.py:37
  168.4 7.6 %all-to-all-done.6 = bf16[8,8,4608]{2,1,0:T(8,128)(2,1)} async-done(((bf16[8,8,4608]{2,1,0:T(8,128)(2,1)}), bf16[8,8,4608]{2,1,0:T(8,128)(2,1)}, u32[]{:S(2)}, u32[]{:S(2)}) %all-to-all-start.6) | async-done | bytes 589856 | tf_op jit(solution)/shard_map/all_to_all | solution.py:17
  208.7 6.5 %all-to-all-done.5 = bf16[8,8,4608]{2,1,0:T(8,128)(2,1)} async-done(((bf16[8,8,4608]{2,1,0:T(8,128)(2,1)}), bf16[8,8,4608]{2,1,0:T(8,128)(2,1)}, u32[]{:S(2)}, u32[]{:S(2)}) %all-to-all-start.5) | async-done | bytes 589856 | tf_op jit(solution)/shard_map/all_to_all | solution.py:31
  221.7 6.0 collective-permute-done.1
  238.0 8.0 %all-to-all-done.10 = bf16[8,8,4608]{2,1,0:T(8,128)(2,1)} async-done(((bf16[8,8,4608]{2,1,0:T(8,128)(2,1)}), bf16[8,8,4608]{2,1,0:T(8,128)(2,1)}, u32[]{:S(2)}, u32[]{:S(2)}) %all-to-all-start.10) | async-done | bytes 589856 | tf_op jit(solution)/shard_map/all_to_all | solution.py:17
  295.1 7.2 %all-to-all-done.9 = bf16[8,8,4608]{2,1,0:T(8,128)(2,1)} async-done(((bf16[8,8,4608]{2,1,0:T(8,128)(2,1)}), bf16[8,8,4608]{2,1,0:T(8,128)(2,1)}, u32[]{:S(2)}, u32[]{:S(2)}) %all-to-all-start.9) | async-done | bytes 589856 | tf_op jit(solution)/shard_map/all_to_all | solution.py:31
  305.5 10.3 %collective-permute-done.2 = bf16[2,8,4608]{2,1,0:T(8,128)(2,1)S(1)} collective-permute-done((bf16[2,8,4608]{2,1,0:T(8,128)(2,1)S(1)}, bf16[2,8,4608]{2,1,0:T(8,128)(2,1)S(1)}, u32[]{:S(2)}, u32[]{:S(2)}) %collective-permute-start.2) | collective-permute-done | bytes 147488 | tf_op jit(solution)/shard_map/ppermute | solution.py:37
  326.6 9.9 %all-to-all-done.22 = bf16[8,8,9216]{2,1,0:T(8,128)(2,1)} async-done(((bf16[8,8,9216]{2,1,0:T(8,128)(2,1)}), bf16[8,8,9216]{2,1,0:T(8,128)(2,1)}, u32[]{:S(2)}, u32[]{:S(2)}) %all-to-all-start.22) | async-done | bytes 1179680 | tf_op jit(solution)/shard_map/all_to_all | solution.py:17
  345.7 10.7 %all-to-all-done.20 = bf16[8,8,9216]{2,1,0:T(8,128)(2,1)} async-done(((bf16[8,8,9216]{2,1,0:T(8,128)(2,1)}), bf16[8,8,9216]{2,1,0:T(8,128)(2,1)}, u32[]{:S(2)}, u32[]{:S(2)}) %all-to-all-start.20) | async-done | bytes 1179680 | tf_op jit(solution)/shard_map/all_to_all | solution.py:17
  363.9 6.5 %all-to-all-done.23 = bf16[8,8,4608]{2,1,0:T(8,128)(2,1)} async-done(((bf16[8,8,4608]{2,1,0:T(8,128)(2,1)}), bf16[8,8,4608]{2,1,0:T(8,128)(2,1)}, u32[]{:S(2)}, u32[]{:S(2)}) %all-to-all-start.23) | async-done | bytes 589856 | tf_op jit(solution)/shard_map/all_to_all | solution.py:31
  376.1 6.5 %all-to-all-done.21 = bf16[8,8,4608]{2,1,0:T(8,128)(2,1)} async-done(((bf16[8,8,4608]{2,1,0:T(8,128)(2,1)}), bf16[8,8,4608]{2,1,0:T(8,128)(2,1)}, u32[]{:S(2)}, u32[]{:S(2)}) %all-to-all-start.21) | async-done | bytes 589856 | tf_op jit(solution)/shard_map/all_to_all | solution.py:31
  387.1 7.5 %collective-permute-start.4 = (bf16[2,8,4608]{2,1,0:T(8,128)(2,1)}, bf16[2,8,4608]{2,1,0:T(8,128)(2,1)}, u32[]{:S(2)}, u32[]{:S(2)}) collective-permute-start(bf16[2,8,4608]{2,1,0:T(8,128)(2,1)} %pad_maximum_fusion.8), channel_id=1, source_target_pairs={{0,248},{8,0},{16,8},{24,16},{32,24},{40,32},{48,40},{56,48},{64,5... | collective-permute-start | bytes 442376 | tf_op jit(solution)/shard_map/ppermute | solution.py:37
  401.7 5.8 all-to-all-done.14
  413.8 10.8 %all-to-all-done.26 = bf16[8,8,9216]{2,1,0:T(8,128)(2,1)} async-done(((bf16[8,8,9216]{2,1,0:T(8,128)(2,1)}), bf16[8,8,9216]{2,1,0:T(8,128)(2,1)}, u32[]{:S(2)}, u32[]{:S(2)}) %all-to-all-start.26) | async-done | bytes 1179680 | tf_op jit(solution)/shard_map/all_to_all | solution.py:17
  484.7 9.5 %collective-permute-start.5 = (bf16[2,8,4608]{2,1,0:T(8,128)(2,1)S(1)}, bf16[2,8,4608]{2,1,0:T(8,128)(2,1)S(1)}, u32[]{:S(2)}, u32[]{:S(2)}) collective-permute-start(bf16[2,8,4608]{2,1,0:T(8,128)(2,1)S(1)} %pad_maximum_fusion.11), channel_id=1, source_target_pairs={{0,248},{8,0},{16,8},{24,16},{32,24},{40,32},{48,40},{56,48},{64,5... | collective-permute-start | bytes 442376 | tf_op jit(solution)/shard_map/ppermute | solution.py:37
  500.2 5.8 all-to-all-start.30
  506.7 11.2 %all-to-all-done.30 = bf16[8,8,9216]{2,1,0:T(8,128)(2,1)} async-done(((bf16[8,8,9216]{2,1,0:T(8,128)(2,1)}), bf16[8,8,9216]{2,1,0:T(8,128)(2,1)}, u32[]{:S(2)}, u32[]{:S(2)}) %all-to-all-start.30) | async-done | bytes 1179680 | tf_op jit(solution)/shard_map/all_to_all | solution.py:17
  606.2 5.8 all-to-all-done.12
  620.1 7.0 %all-to-all-done.13 = bf16[8,8,4608]{2,1,0:T(8,128)(2,1)S(1)} async-done(((bf16[8,8,4608]{2,1,0:T(8,128)(2,1)}), bf16[8,8,4608]{2,1,0:T(8,128)(2,1)S(1)}, u32[]{:S(2)}, u32[]{:S(2)}) %all-to-all-start.13) | async-done | bytes 589856 | tf_op jit(solution)/shard_map/all_to_all | solution.py:31
  (339 shorter events, 389.6 us)
Async XLA Ops:
  19.3 21.6 %all-to-all-start.18 = ((bf16[8,8,9216]{2,1,0:T(8,128)(2,1)}), bf16[8,8,9216]{2,1,0:T(8,128)(2,1)S(1)}, u32[]{:S(2)}, u32[]{:S(2)}) async-start(bf16[8,8,9216]{2,1,0:T(8,128)(2,1)} %broadcast_in_dim.123), calls=%async_computation.18 | async-start | bytes 2359296 | tf_op jit(solution)/shard_map/all_to_all | solution.py:17
  43.0 20.8 %all-to-all-start.16 = ((bf16[8,8,9216]{2,1,0:T(8,128)(2,1)}), bf16[8,8,9216]{2,1,0:T(8,128)(2,1)}, u32[]{:S(2)}, u32[]{:S(2)}) async-start(bf16[8,8,9216]{2,1,0:T(8,128)(2,1)} %broadcast_in_dim.122), calls=%async_computation.16 | async-start | bytes 2359296 | tf_op jit(solution)/shard_map/all_to_all | solution.py:17
  63.8 14.3 %all-to-all-start.19 = ((bf16[8,8,4608]{2,1,0:T(8,128)(2,1)}), bf16[8,8,4608]{2,1,0:T(8,128)(2,1)}, u32[]{:S(2)}, u32[]{:S(2)}) async-start(bf16[8,8,4608]{2,1,0:T(8,128)(2,1)} %fusion.13), calls=%async_computation.19 | async-start | bytes 1179648 | tf_op jit(solution)/shard_map/all_to_all | solution.py:31
  78.0 13.8 %all-to-all-start.17 = ((bf16[8,8,4608]{2,1,0:T(8,128)(2,1)}), bf16[8,8,4608]{2,1,0:T(8,128)(2,1)}, u32[]{:S(2)}, u32[]{:S(2)}) async-start(bf16[8,8,4608]{2,1,0:T(8,128)(2,1)} %fusion.12), calls=%async_computation.17 | async-start | bytes 1179648 | tf_op jit(solution)/shard_map/all_to_all | solution.py:31
  107.7 13.7 %all-to-all-start.2 = ((bf16[8,8,4608]{2,1,0:T(8,128)(2,1)}), bf16[8,8,4608]{2,1,0:T(8,128)(2,1)}, u32[]{:S(2)}, u32[]{:S(2)}) async-start(bf16[8,8,4608]{2,1,0:T(8,128)(2,1)} %broadcast_in_dim.112), calls=%async_computation.2 | async-start | bytes 1179648 | tf_op jit(solution)/shard_map/all_to_all | solution.py:17
  121.4 12.9 %all-to-all-start.1 = ((bf16[8,8,4608]{2,1,0:T(8,128)(2,1)}), bf16[8,8,4608]{2,1,0:T(8,128)(2,1)}, u32[]{:S(2)}, u32[]{:S(2)}) async-start(bf16[8,8,4608]{2,1,0:T(8,128)(2,1)} %fusion.4), calls=%async_computation.1 | async-start | bytes 1179648 | tf_op jit(solution)/shard_map/all_to_all | solution.py:31
  232.3 13.7 %all-to-all-start.10 = ((bf16[8,8,4608]{2,1,0:T(8,128)(2,1)}), bf16[8,8,4608]{2,1,0:T(8,128)(2,1)}, u32[]{:S(2)}, u32[]{:S(2)}) async-start(bf16[8,8,4608]{2,1,0:T(8,128)(2,1)} %broadcast_in_dim.116), calls=%async_computation.10 | async-start | bytes 1179648 | tf_op jit(solution)/shard_map/all_to_all | solution.py:17
  247.8 25.1 %all-to-all-start.8 = ((bf16[8,8,4608]{2,1,0:T(8,128)(2,1)}), bf16[8,8,4608]{2,1,0:T(8,128)(2,1)}, u32[]{:S(2)}, u32[]{:S(2)}) async-start(bf16[8,8,4608]{2,1,0:T(8,128)(2,1)} %broadcast_in_dim.115), calls=%async_computation.8 | async-start | bytes 1179648 | tf_op jit(solution)/shard_map/all_to_all | solution.py:17
  272.9 15.6 %all-to-all-start.11 = ((bf16[8,8,4608]{2,1,0:T(8,128)(2,1)}), bf16[8,8,4608]{2,1,0:T(8,128)(2,1)}, u32[]{:S(2)}, u32[]{:S(2)}) async-start(bf16[8,8,4608]{2,1,0:T(8,128)(2,1)} %fusion.9), calls=%async_computation.11 | async-start | bytes 1179648 | tf_op jit(solution)/shard_map/all_to_all | solution.py:31
  288.5 13.8 %all-to-all-start.9 = ((bf16[8,8,4608]{2,1,0:T(8,128)(2,1)}), bf16[8,8,4608]{2,1,0:T(8,128)(2,1)}, u32[]{:S(2)}, u32[]{:S(2)}) async-start(bf16[8,8,4608]{2,1,0:T(8,128)(2,1)} %fusion.8), calls=%async_computation.9 | async-start | bytes 1179648 | tf_op jit(solution)/shard_map/all_to_all | solution.py:31
  321.5 15.0 %all-to-all-start.22 = ((bf16[8,8,9216]{2,1,0:T(8,128)(2,1)}), bf16[8,8,9216]{2,1,0:T(8,128)(2,1)}, u32[]{:S(2)}, u32[]{:S(2)}) async-start(bf16[8,8,9216]{2,1,0:T(8,128)(2,1)} %broadcast_in_dim.127), calls=%async_computation.22 | async-start | bytes 2359296 | tf_op jit(solution)/shard_map/all_to_all | solution.py:17
  337.6 18.8 %all-to-all-start.20 = ((bf16[8,8,9216]{2,1,0:T(8,128)(2,1)}), bf16[8,8,9216]{2,1,0:T(8,128)(2,1)}, u32[]{:S(2)}, u32[]{:S(2)}) async-start(bf16[8,8,9216]{2,1,0:T(8,128)(2,1)} %broadcast_in_dim.126), calls=%async_computation.20 | async-start | bytes 2359296 | tf_op jit(solution)/shard_map/all_to_all | solution.py:17
  356.4 14.0 %all-to-all-start.23 = ((bf16[8,8,4608]{2,1,0:T(8,128)(2,1)}), bf16[8,8,4608]{2,1,0:T(8,128)(2,1)}, u32[]{:S(2)}, u32[]{:S(2)}) async-start(bf16[8,8,4608]{2,1,0:T(8,128)(2,1)} %fusion.15), calls=%async_computation.23 | async-start | bytes 1179648 | tf_op jit(solution)/shard_map/all_to_all | solution.py:31
  408.6 16.1 %all-to-all-start.26 = ((bf16[8,8,9216]{2,1,0:T(8,128)(2,1)}), bf16[8,8,9216]{2,1,0:T(8,128)(2,1)}, u32[]{:S(2)}, u32[]{:S(2)}) async-start(bf16[8,8,9216]{2,1,0:T(8,128)(2,1)} %broadcast_in_dim.131), calls=%async_computation.26 | async-start | bytes 2359296 | tf_op jit(solution)/shard_map/all_to_all | solution.py:17
  425.8 18.1 %all-to-all-start.24 = ((bf16[8,8,9216]{2,1,0:T(8,128)(2,1)}), bf16[8,8,9216]{2,1,0:T(8,128)(2,1)}, u32[]{:S(2)}, u32[]{:S(2)}) async-start(bf16[8,8,9216]{2,1,0:T(8,128)(2,1)} %broadcast_in_dim.130), calls=%async_computation.24 | async-start | bytes 2359296 | tf_op jit(solution)/shard_map/all_to_all | solution.py:17
  443.9 13.5 %all-to-all-start.27 = ((bf16[8,8,4608]{2,1,0:T(8,128)(2,1)}), bf16[8,8,4608]{2,1,0:T(8,128)(2,1)}, u32[]{:S(2)}, u32[]{:S(2)}) async-start(bf16[8,8,4608]{2,1,0:T(8,128)(2,1)} %fusion.17), calls=%async_computation.27 | async-start | bytes 1179648 | tf_op jit(solution)/shard_map/all_to_all | solution.py:31
  457.4 17.6 %all-to-all-start.25 = ((bf16[8,8,4608]{2,1,0:T(8,128)(2,1)}), bf16[8,8,4608]{2,1,0:T(8,128)(2,1)}, u32[]{:S(2)}, u32[]{:S(2)}) async-start(bf16[8,8,4608]{2,1,0:T(8,128)(2,1)} %fusion.16), calls=%async_computation.25 | async-start | bytes 1179648 | tf_op jit(solution)/shard_map/all_to_all | solution.py:31
  475.0 22.2 %all-to-all-start.15 = ((bf16[8,8,4608]{2,1,0:T(8,128)(2,1)}), bf16[8,8,4608]{2,1,0:T(8,128)(2,1)}, u32[]{:S(2)}, u32[]{:S(2)}) async-start(bf16[8,8,4608]{2,1,0:T(8,128)(2,1)} %fusion.11), calls=%async_computation.15 | async-start | bytes 1179648 | tf_op jit(solution)/shard_map/all_to_all | solution.py:31
  484.7 13.7 %collective-permute-start.5 = (bf16[2,8,4608]{2,1,0:T(8,128)(2,1)S(1)}, bf16[2,8,4608]{2,1,0:T(8,128)(2,1)S(1)}, u32[]{:S(2)}, u32[]{:S(2)}) collective-permute-start(bf16[2,8,4608]{2,1,0:T(8,128)(2,1)S(1)} %pad_maximum_fusion.11), channel_id=1, source_target_pairs={{0,248},{8,0},{16,8},{24,16},{32,24},{40,32},{48,40},{56,48},{64,5... | collective-permute-start | bytes 442376 | tf_op jit(solution)/shard_map/ppermute | solution.py:37
  500.2 17.7 %all-to-all-start.30 = ((bf16[8,8,9216]{2,1,0:T(8,128)(2,1)}), bf16[8,8,9216]{2,1,0:T(8,128)(2,1)}, u32[]{:S(2)}, u32[]{:S(2)}) async-start(bf16[8,8,9216]{2,1,0:T(8,128)(2,1)} %broadcast_in_dim.135), calls=%async_computation.30 | async-start | bytes 2359296 | tf_op jit(solution)/shard_map/all_to_all | solution.py:17
  519.0 25.3 %all-to-all-start.28 = ((bf16[8,8,9216]{2,1,0:T(8,128)(2,1)}), bf16[8,8,9216]{2,1,0:T(8,128)(2,1)}, u32[]{:S(2)}, u32[]{:S(2)}) async-start(bf16[8,8,9216]{2,1,0:T(8,128)(2,1)} %broadcast_in_dim.134), calls=%async_computation.28 | async-start | bytes 2359296 | tf_op jit(solution)/shard_map/all_to_all | solution.py:17
  544.3 24.5 %all-to-all-start.31 = ((bf16[8,8,4608]{2,1,0:T(8,128)(2,1)}), bf16[8,8,4608]{2,1,0:T(8,128)(2,1)}, u32[]{:S(2)}, u32[]{:S(2)}) async-start(bf16[8,8,4608]{2,1,0:T(8,128)(2,1)} %fusion.19), calls=%async_computation.31 | async-start | bytes 1179648 | tf_op jit(solution)/shard_map/all_to_all | solution.py:31
  568.7 15.3 %all-to-all-start.29 = ((bf16[8,8,4608]{2,1,0:T(8,128)(2,1)}), bf16[8,8,4608]{2,1,0:T(8,128)(2,1)}, u32[]{:S(2)}, u32[]{:S(2)}) async-start(bf16[8,8,4608]{2,1,0:T(8,128)(2,1)} %fusion.18), calls=%async_computation.29 | async-start | bytes 1179648 | tf_op jit(solution)/shard_map/all_to_all | solution.py:31
  598.9 13.2 %all-to-all-start.12 = ((bf16[8,8,4608]{2,1,0:T(8,128)(2,1)}), bf16[8,8,4608]{2,1,0:T(8,128)(2,1)}, u32[]{:S(2)}, u32[]{:S(2)}) async-start(bf16[8,8,4608]{2,1,0:T(8,128)(2,1)} %broadcast_in_dim.117), calls=%async_computation.12 | async-start | bytes 1179648 | tf_op jit(solution)/shard_map/all_to_all | solution.py:17
  (70 other events, 638.9 us)
where the time goes:
time: 634 us; the launch traced here: 628 us
  waiting for transfers between devices  198 us (31%)
  starting transfers between devices  178 us (28%)
  matrix products  106 us (17%)
  other arithmetic  71.8 us (11%)
  between operations  32.1 us (5%)
  local copies, waits for them, and re-layouts  27.5 us (4%)
  blocking collectives  13.6 us (2%)
    all_to_all x16, waiting for transfers between devices, copy_for_each(): return lax.all_to_all(copies, axis, split_axis=0, concat_axis=0, tiled=True)  111 us
    all_to_all x16, starting transfers between devices, sum_at_owner(): lax.all_to_all(tiles, axis, split_axis=0, concat_axis=0, tiled=True)  81 us
    all_to_all x16, starting transfers between devices, copy_for_each(): return lax.all_to_all(copies, axis, split_axis=0, concat_axis=0, tiled=True)  79.9 us
    all_to_all x16, waiting for transfers between devices, sum_at_owner(): lax.all_to_all(tiles, axis, split_axis=0, concat_axis=0, tiled=True)  61.7 us
    dot_general x16, matrix products, transposed_times(): lax.dot_general(left, right, (((0,), (0,)), ((), ())), preferred_element_...  57.1 us
    dot_general x16, matrix products, times_transposed(): lax.dot_general(left, right, (((1,), (1,)), ((), ())), preferred_element_...  26.1 us
    ppermute x6, waiting for transfers between devices, shifted(): lax.ppermute(shard, axis, [(i, (i + by) % devices) for i in range(devices)])  25.1 us
    dot_general x8, matrix products, forward(): jnp.dot(values, out_mats[group], preferred_element_type=jnp.float32)  23.2 us
  transfers between devices with their start and end apart: 38, of which 28 were waited for; matrix products, arithmetic and copies ran while one was open for 23% of the time, Pallas kernels for 0%

commit v1 on v0

v1 whole, which is shorter than its diff:
```python
import functools

import jax
import jax.numpy as jnp
from jax import lax
from jax.experimental import pallas as pl
from jax.experimental.pallas import tpu as pltpu
from jax.sharding import PartitionSpec as P

epsilon = 1e-06
MESH = pl.DeviceIdType.MESH
F32, BF16 = jnp.float32, jnp.bfloat16

F0, F1, B0, B1 = range(4)
YN, ZN = 4, 2


def dot_nn(a, b):
    return jnp.dot(a, b, preferred_element_type=F32)


def dot_nt(a, b):
    return lax.dot_general(a, b, (((1,), (1,)), ((), ())), preferred_element_type=F32)


def dot_tn(a, b):
    return lax.dot_general(a, b, (((0,), (0,)), ((), ())), preferred_element_type=F32)


def window(
    n_section,
    wv, wo, gain, saved, arr, ret, fresh, tgt, fill, read,
    act, cot, stash, gv, go, gg,
    nrm, cotf, nsv, xin, part, rsy, keep, zs, zr, ysnd, dsnd, shf, shb, dgs, gacc, gsum,
    ag_s, ag_r, rs_s, rs_r, sh_s, sh_r,
):
    ticks = fresh.shape[0]
    slots = saved.shape[0]
    depth = gain.shape[1]
    rows = arr.shape[1]
    tokens = rows * YN * ZN
    me = lax.axis_index("dp")
    sec = lax.axis_index("section")
    z, y = me // YN, me % YN
    zp = 1 - z
    first = sec == 0
    last = sec == n_section - 1
    nxt = lax.rem(sec + 1, n_section)
    prv = lax.rem(sec + n_section - 1, n_section)
    z_peer = {"dp": zp * YN + y}

    def y_at(k):
        return lax.rem(y + k, YN)

    def y_peer(k):
        return {"dp": z * YN + y_at(k)}

    barrier = pltpu.get_barrier_semaphore()
    for target in (y_peer(1), y_peer(2), y_peer(3), z_peer, {"section": nxt}, {"section": prv}):
        pl.semaphore_signal(barrier, inc=1, device_id=target, device_id_type=MESH)

    def send(src, dst, s, r, target):
        return pltpu.make_async_remote_copy(
            src_ref=src, dst_ref=dst, send_sem=s, recv_sem=r, device_id=target, device_id_type=MESH
        )

    def ag_own(buf, row, k):
        return send(buf.at[me], buf.at[me], ag_s.at[row, k], ag_r.at[row, me], y_peer(k) if k else z_peer)

    def ag_pass(buf, row, k):
        o = z * YN + y_at(k)
        return send(buf.at[o], buf.at[o], ag_s.at[row, YN - 1 + k], ag_r.at[row, o], z_peer)

    def ag_start(buf, row):
        for k in (2, 1, 3, 0):
            ag_own(buf, row, k).start()

    def ag_relay(buf, row):
        for k in (1, 3, 2):
            copy = ag_pass(buf, row, k)
            copy.wait_recv()
            copy.start()

    def ag_finish(buf, row):
        for k in (0, 1, 3, 2):
            o = zp * YN + y_at(k)
            send(buf.at[o], buf.at[o], ag_s.at[row, 0], ag_r.at[row, o], z_peer).wait_recv()

    def ag_drain(buf, row):
        for k in range(YN):
            ag_own(buf, row, k).wait_send()
        for k in range(1, YN):
            ag_pass(buf, row, k).wait_send()

    def rs_y(st, k):
        return send(part.at[st, :, y_at(k)], rsy.at[st, y], rs_s.at[st, k], rs_r.at[st, y], y_peer(k))

    def rs_z(st):
        return send(zs.at[st], zr.at[st], rs_s.at[st, 0], rs_r.at[st, YN], z_peer)

    def shift(st, t):
        g = st % 2
        if st < B0:
            return send(ysnd.at[t, g], shf.at[t, g], sh_s.at[t, st], sh_r.at[t, st], {"section": nxt})
        return send(dsnd.at[t, g], shb.at[t, g], sh_s.at[t, st], sh_r.at[t, st], {"section": prv})

    def normed_of(x, g):
        inv = lax.rsqrt(jnp.mean(x * x, axis=-1, keepdims=True) + epsilon)
        scaled = x * inv
        return scaled, inv, (scaled * gain[g : g + 1, :]).astype(BF16)

    def whole(ref, i):
        return ref[i].astype(F32).reshape(tokens, depth).astype(BF16)

    def buf_of(st, t):
        g = st % 2
        return (nrm if st < B0 else cotf).at[2 * t + g]

    def stage_s(st, t):
        g = st % 2
        if t > 0:
            shift(st, t - 1).wait_recv()
        if st < B0:
            if t == 0:
                x = arr[g].astype(F32)
            else:
                edge = fresh[t] if g == 0 else shf[t - 1, 0]
                x = jnp.where(first, edge.astype(F32), shf[t - 1, g].astype(F32))
            xin[t, g] = x.astype(BF16)
            own = normed_of(x, g)[2]
        elif t == 0:
            own = ret[g]
        else:
            if g == 0:
                edge = shb[t - 1, 1].astype(F32)
            else:
                edge = ysnd[t - 1, 1].astype(F32) - tgt[t - 1].astype(F32)
            own = jnp.where(last, edge, shb[t - 1, g].astype(F32)).astype(BF16)
        if t > 0:
            ag_drain(buf_of(st, t - 1), st)
        buf = buf_of(st, t)
        buf[me] = own
        ag_start(buf, st)

    def stage_relay(st, t):
        ag_relay(buf_of(st, t), st)

    def stage_c(st, t):
        g = st % 2
        ag_finish(buf_of(st, t), st)
        if st < B0:
            values = dot_nn(whole(nrm, 2 * t + g), wv[g]).astype(BF16)
            terms = dot_nn(values, wo[g])
        else:
            down = dot_nt(whole(cotf, 2 * t + g), wo[g]).astype(BF16)
            dgs[g, t * tokens : (t + 1) * tokens, :] = down
            terms = dot_nt(down, wv[g])
        if t > 0:
            for k in range(1, YN):
                rs_y(st, k).wait_send()
        part[st] = terms.reshape(ZN, YN, rows, depth).astype(BF16)
        for k in (2, 1, 3):
            rs_y(st, k).start()

    def stage_y(st, t):
        for k in (1, 3, 2):
            q = y_at(k)
            send(part.at[st, :, q], rsy.at[st, q], rs_s.at[st, k], rs_r.at[st, q], y_peer(k)).wait_recv()

        def total(zz):
            acc = part[st, zz, y].astype(F32)
            for k in range(1, YN):
                acc = acc + rsy[st, y_at(k), zz].astype(F32)
            return acc

        if t > 0:
            rs_z(st).wait_send()
        zs[st] = total(zp).astype(BF16)
        rs_z(st).start()
        keep[st] = total(z)

    def pick(candidates, which):
        chosen = candidates[0][1]
        for index, value in candidates[1:]:
            chosen = jnp.where(index == which, value, chosen)
        return chosen

    def source_rows(t, g):
        options = [(sl, saved[sl, g].astype(F32)) for sl in range(slots)]
        options += [(fill[u, g], xin[u, g].astype(F32)) for u in range(t + 1)]
        return pick(options, read[t, g])

    def stage_e(st, t):
        g = st % 2
        rs_z(st).wait_recv()
        total = keep[st] + zr[st].astype(F32)
        if st < B0:
            out = (xin[t, g].astype(F32) + total).astype(BF16)
            ysnd[t, g] = out
        else:
            scaled, inv, _ = normed_of(source_rows(t, g), g)
            weighted = total * gain[g : g + 1, :]
            inner = jnp.mean(weighted * scaled, axis=-1, keepdims=True)
            upstream = cotf[2 * t + g, me].astype(F32)
            out = (upstream + inv * (weighted - scaled * inner)).astype(BF16)
            dsnd[t, g] = out
            term = total * scaled
            gacc[g] = term if t == 0 else gacc[g] + term
        if t < ticks - 1:
            shift(st, t).start()
        elif st < B0:
            act[g] = out
        else:
            cot[g] = out

    init_items = [(sl, g) for g in range(2) for sl in range(slots)]

    def init_start(i):
        sl, g = init_items[i]
        buf = nsv.at[sl, g]
        buf[me] = normed_of(saved[sl, g].astype(F32), g)[2]
        ag_start(buf, 4 + i)

    def init_relay(i):
        sl, g = init_items[i]
        ag_relay(nsv.at[sl, g], 4 + i)

    def init_finish(i):
        sl, g = init_items[i]
        ag_finish(nsv.at[sl, g], 4 + i)

    def weight_pass(g):
        picked = []
        for t in range(ticks):
            options = [(sl, nsv[sl, g].astype(F32)) for sl in range(slots)]
            options += [(fill[u, g], nrm[2 * u + g].astype(F32)) for u in range(t + 1)]
            picked.append(pick(options, read[t, g]).reshape(tokens, depth).astype(BF16))
        normed = jnp.concatenate(picked, axis=0)
        values = dot_nn(normed, wv[g]).astype(BF16)
        gv[g] = dot_tn(normed, dgs[g]).astype(BF16)
        upstream = jnp.concatenate([whole(cotf, 2 * t + g) for t in range(ticks)], axis=0)
        go[g] = dot_tn(values, upstream).astype(BF16)

    def stash_rows():
        for sl in range(slots):
            for g in range(2):
                rows_now = saved[sl, g].astype(F32)
                for t in range(ticks):
                    rows_now = jnp.where(fill[t, g] == sl, xin[t, g].astype(F32), rows_now)
                stash[sl, g] = rows_now.astype(BF16)

    gain_row = 4 + len(init_items)
    order = (F0, F1, B1, B0)
    pl.semaphore_wait(barrier, 6)
    for st in order:
        stage_s(st, 0)
    for t in range(ticks):
        final = t == ticks - 1
        a, b, c, d = order
        stage_relay(a, t)
        stage_relay(b, t)
        stage_c(a, t)
        stage_relay(c, t)
        stage_c(b, t)
        stage_y(a, t)
        stage_relay(d, t)
        stage_c(c, t)
        if not final:
            init_start(2 * t)
        stage_y(b, t)
        stage_e(a, t)
        stage_c(d, t)
        if not final:
            init_relay(2 * t)
            init_start(2 * t + 1)
        stage_y(c, t)
        stage_e(b, t)
        if not final:
            stage_s(a, t + 1)
            init_relay(2 * t + 1)
        else:
            for i in range(len(init_items)):
                init_finish(i)
            weight_pass(0)
        stage_y(d, t)
        stage_e(c, t)
        if not final:
            stage_s(b, t + 1)
        stage_e(d, t)
        if not final:
            stage_s(c, t + 1)
            stage_s(d, t + 1)
    for g in range(2):
        gsum[me, g : g + 1, :] = jnp.sum(gacc[g], axis=0, keepdims=True)
    ag_start(gsum, gain_row)
    weight_pass(1)
    ag_relay(gsum, gain_row)
    stash_rows()
    ag_finish(gsum, gain_row)
    gg[...] = jnp.sum(gsum[...], axis=0)[0:2, :] * (tokens * ticks) ** (-0.5)
    for st in order:
        ag_drain(buf_of(st, ticks - 1), st)
        for k in range(1, YN):
            rs_y(st, k).wait_send()
        rs_z(st).wait_send()
        for t in range(ticks - 1):
            shift(st, t).wait_send()
    for i, (sl, g) in enumerate(init_items):
        ag_drain(nsv.at[sl, g], 4 + i)
    ag_drain(gsum, gain_row)


def body(n_section, *args):
    w_value, w_out, norm_gain, saved, arriving, returning, fresh, targets, fill, read = args
    wv, wo, gain, saved, arr, ret, fill, read = (
        a[0] for a in (w_value, w_out, norm_gain, saved, arriving, returning, fill, read)
    )
    ticks, rows, depth = fresh.shape
    slots = saved.shape[0]
    feats = wv.shape[2]
    tokens = rows * YN * ZN
    vmem = pl.BlockSpec(memory_space=pltpu.VMEM)
    smem = pl.BlockSpec(memory_space=pltpu.SMEM)
    block = (rows, depth)
    n_rows = 4 + 2 * slots + 1
    dma = pltpu.SemaphoreType.DMA
    outs = pl.pallas_call(
        functools.partial(window, n_section),
        out_shape=(
            jax.ShapeDtypeStruct((2, *block), BF16),
            jax.ShapeDtypeStruct((2, *block), BF16),
            jax.ShapeDtypeStruct((slots, 2, *block), BF16),
            jax.ShapeDtypeStruct(wv.shape, BF16),
            jax.ShapeDtypeStruct(wo.shape, BF16),
            jax.ShapeDtypeStruct((2, depth), F32),
        ),
        in_specs=[vmem] * 8 + [smem] * 2,
        out_specs=[vmem] * 6,
        scratch_shapes=[
            pltpu.VMEM((2 * ticks, 8, *block), BF16),
            pltpu.VMEM((2 * ticks, 8, *block), BF16),
            pltpu.VMEM((slots, 2, 8, *block), BF16),
            pltpu.VMEM((ticks, 2, *block), BF16),
            pltpu.VMEM((4, ZN, YN, *block), BF16),
            pltpu.VMEM((4, YN, ZN, *block), BF16),
            pltpu.VMEM((4, *block), F32),
            pltpu.VMEM((4, *block), BF16),
            pltpu.VMEM((4, *block), BF16),
            pltpu.VMEM((ticks, 2, *block), BF16),
            pltpu.VMEM((ticks, 2, *block), BF16),
            pltpu.VMEM((ticks - 1, 2, *block), BF16),
            pltpu.VMEM((ticks - 1, 2, *block), BF16),
            pltpu.VMEM((2, ticks * tokens, feats), BF16),
            pltpu.VMEM((2, *block), F32),
            pltpu.VMEM((8, 2, depth), F32),
            dma((n_rows, 2 * YN)),
            dma((n_rows, 8)),
            dma((4, YN)),
            dma((4, YN + 1)),
            dma((ticks - 1, 4)),
            dma((ticks - 1, 4)),
        ],
        compiler_params=pltpu.CompilerParams(
            collective_id=0, has_side_effects=True, vmem_limit_bytes=67043328
        ),
        name="window",
    )(wv, wo, gain, saved, arr, ret, fresh, targets, fill, read)
    act, cot, stash, gv, go, gg = outs
    scale = jnp.asarray((ticks * tokens) ** (-0.5), F32)
    gv = (gv.astype(F32) * scale).astype(BF16)
    go = (go.astype(F32) * scale).astype(BF16)
    return tuple(a[None] for a in (act, cot, stash, gv, go, gg))


def solution(mesh):
    in_specs = (
        P("section", None, None, "dp"),
        P("section", None, "dp", None),
        P("section", None, None),
        P("section", None, None, "dp", None),
        P("section", None, "dp", None),
        P("section", None, "dp", None),
        P(None, "dp", None),
        P(None, "dp", None),
        P("section", None, None),
        P("section", None, None),
    )
    out_specs = (
        P("section", None, "dp", None),
        P("section", None, "dp", None),
        P("section", None, None, "dp", None),
        P("section", None, None, "dp"),
        P("section", None, "dp", None),
        P("section", None, None),
    )
    return jax.shard_map(
        functools.partial(body, mesh.shape["section"]),
        mesh=mesh,
        in_specs=in_specs,
        out_specs=out_specs,
        check_vma=False,
    )
```

time: 634 us -> 242 us (0.38)
  Pallas kernels: 0 us -> 226 us
  waiting for transfers between devices: 198 us -> 0 us
  starting transfers between devices: 178 us -> 0 us
  matrix products: 106 us -> 0 us
  other arithmetic: 71.8 us -> 5.47 us
  between operations: 32.1 us -> 0.67 us
  local copies, waits for them, and re-layouts: 27.5 us -> 5.39 us
  blocking collectives: 13.6 us -> 0 us
    pallas_call x0 -> x1, Pallas kernels: none -> 226 us  [body(): pl.pallas_call(functools.partial(window, n_section), out_shape=(jax.Shape...]
    all_to_all x32 -> x0, waiting for transfers between devices: 173 us -> none  [the longest x16 111 us: copy_for_each(): return lax.all_to_all(copies, axis, split_axis=0, concat_axis=0, tiled=True)]
    all_to_all x32 -> x0, starting transfers between devices: 161 us -> none  [the longest x16 81 us: sum_at_owner(): lax.all_to_all(tiles, axis, split_axis=0, concat_axis=0, tiled=True)]
    dot_general x40 -> x0, matrix products: 106 us -> none  [the longest x16 57.1 us: transposed_times(): lax.dot_general(left, right, (((0,), (0,)), ((), ())), preferred_element_...]
    ppermute x6 -> x0, waiting for transfers between devices: 25.1 us -> none  [shifted(): lax.ppermute(shard, axis, [(i, (i + by) % devices) for i in range(devices)])]
    reduce_sum x31 -> x0, other arithmetic: 24.1 us -> none  [the longest x16 18.4 us: sum_at_owner(): return arrived.astype(jnp.float32).sum(axis=0)]
    convert_element_type x20 -> x0, other arithmetic: 19.7 us -> none  [the longest x4 5.01 us: body(): fresh_grads.append((cotangents[group].astype(jnp.float32) + inv_root * (w...]
    ppermute x6 -> x0, starting transfers between devices: 17.4 us -> none  [shifted(): lax.ppermute(shard, axis, [(i, (i + by) % devices) for i in range(devices)])]
  transfers between devices with their start and end apart: 38 -> 0, of which waited for: 28 -> 0; matrix products, arithmetic and copies ran while one was open for 23% -> 0% of each run, Pallas kernels for 0% -> 0%
where the time goes in v1:
time: 242 us; the launch traced here: 238 us
  Pallas kernels  226 us (93%)
  other arithmetic  5.47 us (2%)
  local copies, waits for them, and re-layouts  5.39 us (2%)
    pallas_call x1, Pallas kernels, body(): pl.pallas_call(functools.partial(window, n_section), out_shape=(jax.Shape...  226 us
    broadcast_in_dim x2, other arithmetic, body(): return tuple((a[None] for a in (act, cot, stash, gv, go, gg)))  5.47 us

profile of v1, /device:TPU:32, one launch (start us, length us, event | category | flops | bytes accessed | tf_op | source)
XLA Modules:
  0.0 237.6 jit_solution(6379222952520508806)
XLA Ops:
  0.6 1.3 copy.16.fill
  2.0 1.3 copy.17.read
  3.3 226.1 %window.1 = (bf16[2,8,4608]{2,1,0:T(8,128)(2,1)}, bf16[2,8,4608]{2,1,0:T(8,128)(2,1)}, bf16[3,2,8,4608]{3,2,1,0:T(8,128)(2,1)}, bf16[2,4608,128]{2,1,0:T(8,128)(...) custom-call(bf16[2,4608,128]{2,1,0:T(8,128)(2,1)} %bitcast.16, bf16[2,128,4608]{2,1,0:T(8,128)(2,1)} %bitcast.17, ...), custom_call_target="tpu_custom_call" | custom-call | tf_op jit(solution)/shard_map/window/pallas_call | solution.py:327
  229.4 0.0 copy-start
  229.4 3.7 %fusion = bf16[1,2,4608,128]{3,2,1,0:T(8,128)(2,1)} fusion(bf16[2,4608,128]{2,1,0:T(8,128)(2,1)} %get-tuple-element.15), kind=kLoop, calls=%fused_computation.2 | loop fusion | flops 3538944 | bytes 4718592 | tf_op jit(solution)/shard_map/broadcast_in_dim | solution.py:372
  233.1 0.0 copy-done
  233.1 0.0 copy-start.3
  233.1 0.0 copy-start.2
  233.1 0.0 copy-start.1
  233.1 0.0 copy-start.4
  233.1 1.8 fusion.1
  234.9 0.0 copy-done.3
  234.9 0.7 copy.22
  235.5 0.0 copy-done.2
  235.5 0.7 copy.23
  236.2 0.0 copy-done.1
  236.2 0.8 copy.24
  237.0 0.0 copy-done.4
  237.0 0.6 copy.25
Async XLA Ops:
  229.4 3.7 %copy-start = (bf16[2,128,4608]{2,1,0:T(8,128)(2,1)S(1)}, bf16[2,128,4608]{2,1,0:T(8,128)(2,1)}, u32[]{:S(2)}) copy-start(bf16[2,128,4608]{2,1,0:T(8,128)(2,1)} %get-tuple-element.16) | copy-start | bytes 7077892
  233.1 1.8 copy-start.3
  233.1 2.5 %copy-start.2 = (bf16[2,8,4608]{2,1,0:T(8,128)(2,1)S(1)}, bf16[2,8,4608]{2,1,0:T(8,128)(2,1)}, u32[]{:S(2)}) copy-start(bf16[2,8,4608]{2,1,0:T(8,128)(2,1)} %get-tuple-element.13) | copy-start | bytes 442372
  233.1 3.1 %copy-start.1 = (bf16[3,2,8,4608]{3,2,1,0:T(8,128)(2,1)S(1)}, bf16[3,2,8,4608]{3,2,1,0:T(8,128)(2,1)}, u32[]{:S(2)}) copy-start(bf16[3,2,8,4608]{3,2,1,0:T(8,128)(2,1)} %get-tuple-element.14) | copy-start | bytes 1327108
  233.1 3.9 %copy-start.4 = (f32[2,4608]{1,0:T(2,128)S(1)}, f32[2,4608]{1,0:T(2,128)}, u32[]{:S(2)}) copy-start(f32[2,4608]{1,0:T(2,128)} %get-tuple-element.17) | copy-start | bytes 110596

commit v2 on v1

v2 whole, which is shorter than its diff:
```python
import functools

import jax
import jax.numpy as jnp
from jax import lax
from jax.experimental import pallas as pl
from jax.experimental.pallas import tpu as pltpu
from jax.sharding import PartitionSpec as P

epsilon = 1e-06
MESH = pl.DeviceIdType.MESH
F32, BF16 = jnp.float32, jnp.bfloat16

F0, F1, B0, B1 = range(4)
YN, ZN = 4, 2

PIECES = {
    "y1": ((0, 0, None), 1),
    "y3": ((0, 0, None), -1),
    "y2": ((0, 0, None), 2),
    "z0": ((0, 0, None), "z"),
    "z1": ((0, -1, None), "z"),
    "z3": ((0, 1, None), "z"),
    "z2": ((0, 2, None), "z"),
    "w1": ((1, 0, None), 1),
    "w3": ((1, 0, None), -1),
    "h1": ((0, -1, 0), 1),
    "h3": ((0, 1, 1), -1),
    "v1": ((1, -1, 0), 1),
    "v3": ((1, 1, 1), -1),
}
GATHERS = {
    "Y": {
        "S": ((), ("y2", "y1", "y3", "z0")),
        "R": (("y1", "y3", "y2"), ("z1", "z3", "z2")),
        "C": (("z0", "z1", "z3", "z2"), ()),
    },
    "YR": {
        "S": ((), ("y1", "y3", "z0")),
        "R": (("y1", "y3"), ("h1", "h3", "z1", "z3")),
        "Q": (("h1", "h3"), ("z2",)),
        "C": (("z0", "z1", "z3", "z2"), ()),
    },
    "ZR": {
        "S": ((), ("z0", "y1", "y3")),
        "R": (("z0", "y1", "y3"), ("w1", "w3", "h1", "h3")),
        "Q": (("w1", "w3"), ("v1", "v3")),
        "C": (("h1", "h3", "v1", "v3"), ()),
    },
}
N_KEYS = 9
STREAM_MODES = (("YR", "yr"), ("ZR", "zr"), ("ZR", "zr"), ("YR", "yr"))
INIT_MODE = "ZR"
ORDER = (
    "S20", "S10", "S00", "S30", "R00", "R10", "R20", "Q00", "R30", "Q10", "Q20", "C00",
    "Q30", "S50", "C10", "C30", "P00", "C20", "Y00", "R50", "P30", "S90", "P20", "P10",
    "E00", "S40", "Y10", "Y30", "S01", "Y20", "E30", "E10", "R40", "R01", "Q50", "E20",
    "S11", "Q01", "S31", "R11", "S21", "R31", "Q11", "R21", "Q31", "C01", "C11", "Q21",
    "C31", "C21", "Q40", "P31", "P01", "P11", "Y31", "Y01", "P21", "Y11", "E31", "R90",
    "E01", "Y21", "S80", "E11", "S32", "S02", "E21", "S12", "R32", "S22", "Q32", "R12",
    "R02", "Q12", "R22", "C32", "Q02", "C12", "Q22", "P32", "Q90", "C22", "C02", "Y32",
    "S60", "P12", "P02", "S70", "P22", "Y02", "Y12", "Y22", "R80", "E32", "R70", "E02",
    "E22", "E12", "S33", "S03", "S23", "S13", "R03", "R23", "R33", "Q23", "R13", "Q80",
    "R60", "Q33", "C23", "Q70", "T00", "C33", "Q03", "Q13", "Q60", "P33", "C13", "P23",
    "C03", "Y23", "P03", "Y33", "W10", "P13", "E23", "E33", "G00", "W00", "Y03", "Y13",
    "H00", "E13", "E03",
)
VMEM_LIMIT = 52428800


def scoped(stage):
    def run(*ids):
        with jax.named_scope("_".join([stage.__name__] + [str(i) for i in ids])):
            return stage(*ids)

    return run


def dot_nn(a, b):
    return jnp.dot(a, b, preferred_element_type=F32)


def dot_nt(a, b):
    return lax.dot_general(a, b, (((1,), (1,)), ((), ())), preferred_element_type=F32)


def dot_tn(a, b):
    return lax.dot_general(a, b, (((0,), (0,)), ((), ())), preferred_element_type=F32)


def window(
    n_section,
    gain, arr, ret, wv_in, wo_in, saved_in, fresh_in, tgt_in, fill, read,
    act, cot, stash, gv, go, gg,
    wv, wo, saved, fresh, tgt,
    nrm, cotf, nsv, xin, part, rsh, rsy, zq, keep, zs, zr, ysnd, dsnd, shf, shb, dgs, gacc, gsum,
    in_s, ag_s, ag_r, rs_s, rs_r, sh_s, sh_r, g_s, g_r,
):
    ticks = fresh.shape[0]
    slots = saved.shape[0]
    depth = gain.shape[1]
    half = depth // 2
    rows = arr.shape[1]
    tokens = rows * YN * ZN
    me = lax.axis_index("dp")
    sec = lax.axis_index("section")
    z, y = me // YN, me % YN
    zp = 1 - z
    first = sec == 0
    last = sec == n_section - 1
    nxt = lax.rem(sec + 1, n_section)
    prv = lax.rem(sec + n_section - 1, n_section)

    def y_at(k):
        return lax.rem(y + k + YN, YN)

    def to(where):
        if where == "z":
            return {"dp": zp * YN + y}
        return {"dp": z * YN + y_at(where)}

    others = [(dz, dy) for dz in range(ZN) for dy in range(YN) if dz or dy]

    def other(dz, dy):
        return (zp if dz else z) * YN + y_at(dy)

    barrier = pltpu.get_barrier_semaphore()
    for target in [{"dp": other(*o)} for o in others] + [{"section": nxt}, {"section": prv}]:
        pl.semaphore_signal(barrier, inc=1, device_id=target, device_id_type=MESH)

    loads = {
        "wv": (wv_in, wv),
        "wo": (wo_in, wo),
        "saved": (saved_in, saved),
        "fresh": (fresh_in, fresh),
        "tgt": (tgt_in, tgt),
    }
    loads = {
        name: pltpu.make_async_copy(src, dst, in_s.at[i]) for i, (name, (src, dst)) in enumerate(loads.items())
    }
    for copy in loads.values():
        copy.start()
    loaded = set()

    def need(*names):
        for name in names:
            if name not in loaded:
                loads[name].wait()
                loaded.add(name)

    def send(src, dst, s, r, target):
        return pltpu.make_async_remote_copy(
            src_ref=src, dst_ref=dst, send_sem=s, recv_sem=r, device_id=target, device_id_type=MESH
        )

    def columns(h):
        return pl.ds(0, depth) if h is None else pl.ds(h * half, half)

    init_items = [(sl, g) for g in range(2) for sl in range(slots)]

    def mode_of(row):
        return STREAM_MODES[row][0] if row < 4 else INIT_MODE

    def buf_of(row, t):
        if row >= 4:
            return nsv.at[init_items[row - 4]]
        return (nrm if row < B0 else cotf).at[2 * t + row % 2]

    def gather_copy(row, t, key, arriving=False):
        (dz, dy, h), where = PIECES[key]
        if arriving:
            dz, dy = (1 - dz, dy) if where == "z" else (dz, dy - where)
        block = buf_of(row, t).at[other(dz, dy), :, columns(h)]
        i = [k for _, sends in GATHERS[mode_of(row)].values() for k in sends].index(key)
        return send(block, block, ag_s.at[row, i], ag_r.at[row, i], to(where))

    def gather(stage, row, t):
        waits, sends = GATHERS[mode_of(row)][stage]
        for key in waits:
            gather_copy(row, t, key, arriving=True).wait_recv()
        for key in sends:
            gather_copy(row, t, key).start()

    def gather_drain(row, t):
        for _, sends in GATHERS[mode_of(row)].values():
            for key in sends:
                gather_copy(row, t, key).wait_send()

    def sum_copy(st, key):
        i = ("h1", "h3", "p1", "p3", "q").index(key)
        over_y = STREAM_MODES[st][1] == "yr"
        if key == "q":
            src, dst = (zs.at[st], zr.at[st]) if over_y else (part.at[st, zp], zq.at[st])
            return send(src, dst, rs_s.at[st, i], rs_r.at[st, i], to("z"))
        zz = pl.ds(0, ZN) if over_y else pl.ds(z, 1)
        way = 1 if key[1] == "1" else -1
        side = 0 if way == 1 else 1
        if key[0] == "h":
            src = part.at[st, zz, y_at(2), :, columns(side)]
            dst = rsh.at[st, side, pl.ds(0, ZN if over_y else 1)]
        else:
            src = part.at[st, zz, y_at(way)]
            dst = rsy.at[st, side, pl.ds(0, ZN if over_y else 1)]
        return send(src, dst, rs_s.at[st, i], rs_r.at[st, i], to(way))

    def sum_wait(st, *keys):
        for key in keys:
            sum_copy(st, key).wait_recv()

    def sum_start(st, *keys):
        for key in keys:
            sum_copy(st, key).start()

    def sum_drain(st):
        for key in ("h1", "h3", "p1", "p3", "q"):
            sum_copy(st, key).wait_send()

    def add_halves(st, zz, slot):
        for side, way in ((0, 1), (1, -1)):
            at = (st, zz, y_at(way), slice(None), columns(side))
            part[at] = (part[at].astype(F32) + rsh[st, side, slot].astype(F32)).astype(BF16)

    def shift(st, t):
        g = st % 2
        if st < B0:
            return send(ysnd.at[t, g], shf.at[t, g], sh_s.at[t, st], sh_r.at[t, st], {"section": nxt})
        return send(dsnd.at[t, g], shb.at[t, g], sh_s.at[t, st], sh_r.at[t, st], {"section": prv})

    def normed_of(x, g):
        inv = lax.rsqrt(jnp.mean(x * x, axis=-1, keepdims=True) + epsilon)
        scaled = x * inv
        return scaled, inv, (scaled * gain[g : g + 1, :]).astype(BF16)

    def whole(ref, i):
        return ref[i].astype(F32).reshape(tokens, depth).astype(BF16)

    @scoped
    def stage_s(st, t):
        if st >= 4:
            need("saved")
            sl, g = init_items[st - 4]
            buf_of(st, t)[me] = normed_of(saved[sl, g].astype(F32), g)[2]
            gather("S", st, t)
            return
        g = st % 2
        if t > 0:
            shift(st, t - 1).wait_recv()
        if st < B0:
            if t == 0:
                x = arr[g].astype(F32)
            else:
                need("fresh")
                edge = fresh[t] if g == 0 else shf[t - 1, 0]
                x = jnp.where(first, edge.astype(F32), shf[t - 1, g].astype(F32))
            xin[t, g] = x.astype(BF16)
            own = normed_of(x, g)[2]
        elif t == 0:
            own = ret[g]
        else:
            if g == 0:
                edge = shb[t - 1, 1].astype(F32)
            else:
                need("tgt")
                edge = ysnd[t - 1, 1].astype(F32) - tgt[t - 1].astype(F32)
            own = jnp.where(last, edge, shb[t - 1, g].astype(F32)).astype(BF16)
        if t > 0:
            gather_drain(st, t - 1)
        buf_of(st, t)[me] = own
        gather("S", st, t)

    @scoped
    def stage_r(row, t):
        gather("R", row, t)

    @scoped
    def stage_q(row, t):
        gather("Q", row, t)

    @scoped
    def stage_c(st, t):
        g = st % 2
        gather("C", st, t)
        need("wv", "wo")
        if st < B0:
            values = dot_nn(whole(nrm, 2 * t + g), wv[g]).astype(BF16)
            terms = dot_nn(values, wo[g])
        else:
            down = dot_nt(whole(cotf, 2 * t + g), wo[g]).astype(BF16)
            dgs[g, t * tokens : (t + 1) * tokens, :] = down
            terms = dot_nt(down, wv[g])
        if t > 0:
            sum_drain(st)
        part[st] = terms.reshape(ZN, YN, rows, depth).astype(BF16)
        if STREAM_MODES[st][1] == "yr":
            sum_start(st, "h1", "h3")
        else:
            sum_start(st, "q")

    @scoped
    def stage_p(st, t):
        if STREAM_MODES[st][1] == "yr":
            sum_wait(st, "h1", "h3")
            for zz in range(ZN):
                add_halves(st, zz, zz)
            sum_start(st, "p1", "p3")
        else:
            sum_wait(st, "q")
            for k in (2, 1, 3, 0):
                both = part[st, z, y_at(k)].astype(F32) + zq[st, y_at(k)].astype(F32)
                if k:
                    part[st, z, y_at(k)] = both.astype(BF16)
                else:
                    keep[st] = both
                if k == 2:
                    sum_start(st, "h1", "h3")

    @scoped
    def stage_y(st, t):
        if STREAM_MODES[st][1] == "yr":
            sum_wait(st, "p1", "p3")

            def total(zz):
                acc = part[st, zz, y].astype(F32) + rsy[st, 0, zz].astype(F32)
                return acc + rsy[st, 1, zz].astype(F32)

            zs[st] = total(zp).astype(BF16)
            sum_start(st, "q")
            keep[st] = total(z)
        else:
            sum_wait(st, "h1", "h3")
            add_halves(st, z, 0)
            sum_start(st, "p1", "p3")

    def pick(candidates, which):
        chosen = candidates[0][1]
        for index, value in candidates[1:]:
            chosen = jnp.where(index == which, value, chosen)
        return chosen

    def source_rows(t, g):
        options = [(sl, saved[sl, g].astype(F32)) for sl in range(slots)]
        options += [(fill[0, u, g], xin[u, g].astype(F32)) for u in range(t + 1)]
        return pick(options, read[0, t, g])

    @scoped
    def stage_e(st, t):
        g = st % 2
        if STREAM_MODES[st][1] == "yr":
            sum_wait(st, "q")
            total = keep[st] + zr[st].astype(F32)
        else:
            sum_wait(st, "p1", "p3")
            total = keep[st] + rsy[st, 0, 0].astype(F32) + rsy[st, 1, 0].astype(F32)
        if st < B0:
            out = (xin[t, g].astype(F32) + total).astype(BF16)
            ysnd[t, g] = out
        else:
            need("saved")
            scaled, inv, _ = normed_of(source_rows(t, g), g)
            weighted = total * gain[g : g + 1, :]
            inner = jnp.mean(weighted * scaled, axis=-1, keepdims=True)
            upstream = cotf[2 * t + g, me].astype(F32)
            out = (upstream + inv * (weighted - scaled * inner)).astype(BF16)
            dsnd[t, g] = out
            term = total * scaled
            gacc[g] = term if t == 0 else gacc[g] + term
        if t < ticks - 1:
            shift(st, t).start()
        elif st < B0:
            act[g] = out
        else:
            cot[g] = out

    @scoped
    def stage_w(g, _):
        for i in range(slots):
            gather("C", 4 + g * slots + i, 0)
        picked = []
        for t in range(ticks):
            options = [(sl, nsv[sl, g].astype(F32)) for sl in range(slots)]
            options += [(fill[0, u, g], nrm[2 * u + g].astype(F32)) for u in range(t + 1)]
            picked.append(pick(options, read[0, t, g]).reshape(tokens, depth).astype(BF16))
        normed = jnp.concatenate(picked, axis=0)
        values = dot_nn(normed, wv[g]).astype(BF16)
        gv[g] = dot_tn(normed, dgs[g]).astype(BF16)
        upstream = jnp.concatenate([whole(cotf, 2 * t + g) for t in range(ticks)], axis=0)
        go[g] = dot_tn(values, upstream).astype(BF16)

    @scoped
    def stage_t(_, __):
        for sl in range(slots):
            for g in range(2):
                rows_now = saved[sl, g].astype(F32)
                for t in range(ticks):
                    rows_now = jnp.where(fill[0, t, g] == sl, xin[t, g].astype(F32), rows_now)
                stash[sl, g] = rows_now.astype(BF16)

    def gain_copy(i, arriving=False):
        peer = other(*others[i])
        row = peer if arriving else me
        return send(gsum.at[row], gsum.at[row], g_s.at[i], g_r.at[i], {"dp": peer})

    @scoped
    def stage_g(_, __):
        for g in range(2):
            gsum[me, g : g + 1, :] = jnp.sum(gacc[g], axis=0, keepdims=True)
        for i in range(len(others)):
            gain_copy(i).start()

    @scoped
    def stage_h(_, __):
        for i, (dz, dy) in enumerate(others):
            j = others.index((dz, -dy % YN))
            peer = other(dz, dy)
            send(gsum.at[peer], gsum.at[peer], g_s.at[j], g_r.at[j], {"dp": peer}).wait_recv()
        gg[...] = jnp.sum(gsum[...], axis=0) * (tokens * ticks) ** (-0.5)

    pl.semaphore_wait(barrier, len(others) + 2)
    stages = {
        "S": stage_s, "R": stage_r, "Q": stage_q, "C": stage_c, "P": stage_p, "Y": stage_y,
        "E": stage_e, "W": stage_w, "T": stage_t, "G": stage_g, "H": stage_h,
    }
    for step in ORDER:
        stages[step[0]](int(step[1]), int(step[2]))
    for st in range(4):
        gather_drain(st, ticks - 1)
        sum_drain(st)
        for t in range(ticks - 1):
            shift(st, t).wait_send()
    for i in range(len(init_items)):
        gather_drain(4 + i, 0)
    for i in range(len(others)):
        gain_copy(i).wait_send()


def body(n_section, *args):
    w_value, w_out, norm_gain, saved, arriving, returning, fresh, targets, fill, read = args
    wv, wo, gain, saved, arr, ret = (
        a[0] for a in (w_value, w_out, norm_gain, saved, arriving, returning)
    )
    ticks, rows, depth = fresh.shape
    slots = saved.shape[0]
    feats = wv.shape[2]
    tokens = rows * YN * ZN
    vmem = pl.BlockSpec(memory_space=pltpu.VMEM)
    smem = pl.BlockSpec(memory_space=pltpu.SMEM)
    hbm = pl.BlockSpec(memory_space=pltpu.HBM)
    block = (rows, depth)
    n_rows = 4 + 2 * slots
    dma = pltpu.SemaphoreType.DMA
    held = [pltpu.VMEM(a.shape, a.dtype) for a in (wv, wo, saved, fresh, targets)]
    outs = pl.pallas_call(
        functools.partial(window, n_section),
        out_shape=(
            jax.ShapeDtypeStruct((2, *block), BF16),
            jax.ShapeDtypeStruct((2, *block), BF16),
            jax.ShapeDtypeStruct((slots, 2, *block), BF16),
            jax.ShapeDtypeStruct(wv.shape, BF16),
            jax.ShapeDtypeStruct(wo.shape, BF16),
            jax.ShapeDtypeStruct((2, depth), F32),
        ),
        in_specs=[vmem] * 3 + [hbm] * 5 + [smem] * 2,
        out_specs=[vmem] * 6,
        scratch_shapes=held
        + [
            pltpu.VMEM((2 * ticks, 8, *block), BF16),
            pltpu.VMEM((2 * ticks, 8, *block), BF16),
            pltpu.VMEM((slots, 2, 8, *block), BF16),
            pltpu.VMEM((ticks, 2, *block), BF16),
            pltpu.VMEM((4, ZN, YN, *block), BF16),
            pltpu.VMEM((4, 2, ZN, rows, depth // 2), BF16),
            pltpu.VMEM((4, 2, ZN, *block), BF16),
            pltpu.VMEM((4, YN, *block), BF16),
            pltpu.VMEM((4, *block), F32),
            pltpu.VMEM((4, *block), BF16),
            pltpu.VMEM((4, *block), BF16),
            pltpu.VMEM((ticks, 2, *block), BF16),
            pltpu.VMEM((ticks, 2, *block), BF16),
            pltpu.VMEM((ticks - 1, 2, *block), BF16),
            pltpu.VMEM((ticks - 1, 2, *block), BF16),
            pltpu.VMEM((2, ticks * tokens, feats), BF16),
            pltpu.VMEM((2, *block), F32),
            pltpu.VMEM((8, 2, depth), F32),
            dma((len(held),)),
            dma((n_rows, N_KEYS)),
            dma((n_rows, N_KEYS)),
            dma((4, 5)),
            dma((4, 5)),
            dma((ticks - 1, 4)),
            dma((ticks - 1, 4)),
            dma((7,)),
            dma((7,)),
        ],
        compiler_params=pltpu.CompilerParams(
            collective_id=0, has_side_effects=True, vmem_limit_bytes=VMEM_LIMIT
        ),
        name="window",
    )(gain, arr, ret, wv, wo, saved, fresh, targets, fill, read)
    act, cot, stash, gv, go, gg = outs
    scale = jnp.asarray((ticks * tokens) ** (-0.5), F32)
    gv = (gv.astype(F32) * scale).astype(BF16)
    go = (go.astype(F32) * scale).astype(BF16)
    return tuple(a[None] for a in (act, cot, stash, gv, go, gg))


def solution(mesh):
    in_specs = (
        P("section", None, None, "dp"),
        P("section", None, "dp", None),
        P("section", None, None),
        P("section", None, None, "dp", None),
        P("section", None, "dp", None),
        P("section", None, "dp", None),
        P(None, "dp", None),
        P(None, "dp", None),
        P("section", None, None),
        P("section", None, None),
    )
    out_specs = (
        P("section", None, "dp", None),
        P("section", None, "dp", None),
        P("section", None, None, "dp", None),
        P("section", None, None, "dp"),
        P("section", None, "dp", None),
        P("section", None, None),
    )
    return jax.shard_map(
        functools.partial(body, mesh.shape["section"]),
        mesh=mesh,
        in_specs=in_specs,
        out_specs=out_specs,
        check_vma=False,
    )
```

time: 242 us -> 199 us (0.82); the launches traced: 238 us -> 198 us
  Pallas kernels: 226 us -> 182 us
  local copies, waits for them, and re-layouts: 5.39 us -> 9.75 us
    pallas_call x1, Pallas kernels: 226 us -> 182 us  [body(): pl.pallas_call(functools.partial(window, n_section), out_shape=(jax.Shape...]
    unnamed x14 -> x20, local copies, waits for them, and re-layouts: 2.72 us -> 9.75 us
    squeeze x2 -> x0, local copies, waits for them, and re-layouts: 2.67 us -> none  [body(): a[0]]
where the time goes in v2:
time: 199 us; the launch traced here: 198 us
  Pallas kernels  182 us (91%)
  local copies, waits for them, and re-layouts  9.75 us (5%)
  other arithmetic  5.47 us (3%)
    pallas_call x1, Pallas kernels, body(): pl.pallas_call(functools.partial(window, n_section), out_shape=(jax.Shape...  182 us
    unnamed x20, local copies, waits for them, and re-layouts  9.75 us
    broadcast_in_dim x2, other arithmetic, body(): return tuple((a[None] for a in (act, cot, stash, gv, go, gg)))  5.47 us

profile of v2, /device:TPU:32, one launch (start us, length us, event | category | flops | bytes accessed | tf_op | source)
XLA Modules:
  0.0 198.1 jit_solution(10639453467836907890)
XLA Ops:
  0.6 0.8 copy.16.fill
  1.4 0.8 copy.17.read
  2.2 0.0 copy-start
  2.2 1.0 copy-done
  3.2 0.0 copy-start.1
  3.2 1.0 copy-done.1
  4.1 0.0 copy-start.2
  4.1 1.0 copy-done.2
  5.1 0.0 copy-start.3
  5.1 0.9 copy-done.3
  6.0 0.0 copy-start.4
  6.0 0.9 copy-done.4
  6.9 0.0 copy-start.5
  6.9 0.8 copy-done.5
  7.7 182.2 %window.1 = (bf16[2,8,4608]{2,1,0:T(8,128)(2,1)S(1)}, bf16[2,8,4608]{2,1,0:T(8,128)(2,1)S(1)}, bf16[3,2,8,4608]{3,2,1,0:T(8,128)(2,1)S(1)}, bf16[2,4608,128]{2,1...) custom-call(f32[2,4608]{1,0:T(2,128)S(1)} %bitcast.21, bf16[2,8,4608]{2,1,0:T(8,128)(2,1)S(1)} %bitcast.16, ...), custom_call_target="tpu_custom_call" | custom-call | tf_op jit(solution)/shard_map/window/pallas_call | solution.py:452
  189.9 0.0 copy-start.6
  190.0 3.7 %fusion = bf16[1,2,4608,128]{3,2,1,0:T(8,128)(2,1)} fusion(bf16[2,4608,128]{2,1,0:T(8,128)(2,1)} %get-tuple-element.15), kind=kLoop, calls=%fused_computation.2 | loop fusion | flops 3538944 | bytes 4718592 | tf_op jit(solution)/shard_map/broadcast_in_dim | solution.py:503
  193.6 0.0 copy-done.6
  193.6 1.8 fusion.1
  195.4 0.7 copy.22
  196.1 0.7 copy.23
  196.7 0.8 copy.24
  197.5 0.6 copy.25
Async XLA Ops:
  2.2 1.0 copy-start
  3.2 1.0 copy-start.1
  4.1 1.0 copy-start.2
  5.1 0.9 copy-start.3
  6.0 0.9 copy-start.4
  6.9 0.8 copy-start.5
  189.9 3.7 %copy-start.6 = (bf16[2,128,4608]{2,1,0:T(8,128)(2,1)S(1)}, bf16[2,128,4608]{2,1,0:T(8,128)(2,1)}, u32[]{:S(2)}) copy-start(bf16[2,128,4608]{2,1,0:T(8,128)(2,1)} %get-tuple-element.16) | copy-start | bytes 7077892

commit v3 on v2

--- a/solution.py
+++ b/solution.py
@@ -17,7 +17,6 @@
 PIECES = {
     "y1": ((0, 0, None), 1),
     "y3": ((0, 0, None), -1),
-    "y2": ((0, 0, None), 2),
     "z0": ((0, 0, None), "z"),
     "z1": ((0, -1, None), "z"),
     "z3": ((0, 1, None), "z"),
@@ -29,43 +28,39 @@
     "v1": ((1, -1, 0), 1),
     "v3": ((1, 1, 1), -1),
 }
+KEYS = tuple(PIECES)
 GATHERS = {
     "Y": {
-        "S": ((), ("y2", "y1", "y3", "z0")),
-        "R": (("y1", "y3", "y2"), ("z1", "z3", "z2")),
-        "C": (("z0", "z1", "z3", "z2"), ()),
-    },
-    "YR": {
         "S": ((), ("y1", "y3", "z0")),
         "R": (("y1", "y3"), ("h1", "h3", "z1", "z3")),
         "Q": (("h1", "h3"), ("z2",)),
         "C": (("z0", "z1", "z3", "z2"), ()),
     },
-    "ZR": {
+    "Z": {
         "S": ((), ("z0", "y1", "y3")),
         "R": (("z0", "y1", "y3"), ("w1", "w3", "h1", "h3")),
         "Q": (("w1", "w3"), ("v1", "v3")),
         "C": (("h1", "h3", "v1", "v3"), ()),
     },
 }
-N_KEYS = 9
-STREAM_MODES = (("YR", "yr"), ("ZR", "zr"), ("ZR", "zr"), ("YR", "yr"))
-INIT_MODE = "ZR"
+STREAM_GATHERS = ("YZZY", "ZYYY", "ZYZY", "YZYZ")
+STREAM_SUMS = ("YYYZ", "YYYY", "ZYZY", "YZYY")
+INIT_GATHERS = "ZYZZYZ"
 ORDER = (
-    "S20", "S10", "S00", "S30", "R00", "R10", "R20", "Q00", "R30", "Q10", "Q20", "C00",
-    "Q30", "S50", "C10", "C30", "P00", "C20", "Y00", "R50", "P30", "S90", "P20", "P10",
-    "E00", "S40", "Y10", "Y30", "S01", "Y20", "E30", "E10", "R40", "R01", "Q50", "E20",
-    "S11", "Q01", "S31", "R11", "S21", "R31", "Q11", "R21", "Q31", "C01", "C11", "Q21",
-    "C31", "C21", "Q40", "P31", "P01", "P11", "Y31", "Y01", "P21", "Y11", "E31", "R90",
-    "E01", "Y21", "S80", "E11", "S32", "S02", "E21", "S12", "R32", "S22", "Q32", "R12",
-    "R02", "Q12", "R22", "C32", "Q02", "C12", "Q22", "P32", "Q90", "C22", "C02", "Y32",
-    "S60", "P12", "P02", "S70", "P22", "Y02", "Y12", "Y22", "R80", "E32", "R70", "E02",
-    "E22", "E12", "S33", "S03", "S23", "S13", "R03", "R23", "R33", "Q23", "R13", "Q80",
-    "R60", "Q33", "C23", "Q70", "T00", "C33", "Q03", "Q13", "Q60", "P33", "C13", "P23",
-    "C03", "Y23", "P03", "Y33", "W10", "P13", "E23", "E33", "G00", "W00", "Y03", "Y13",
+    "S00", "S10", "S20", "R00", "S30", "R10", "R20", "Q00", "R30", "Q10", "Q20", "C00",
+    "S80", "Q30", "C10", "C20", "P00", "C30", "P10", "Y00", "P30", "P20", "S50", "E00",
+    "S60", "Y10", "Y30", "Y20", "S01", "E10", "E30", "S70", "E20", "S40", "R01", "S11",
+    "S31", "S21", "R11", "Q01", "R31", "Q11", "R21", "Q31", "C01", "Q21", "C11", "C31",
+    "P01", "C21", "P11", "Y01", "R50", "P31", "P21", "E01", "Y31", "R60", "Y11", "Y21",
+    "E31", "S02", "R70", "E21", "E11", "R80", "R02", "S32", "S22", "S12", "R32", "Q02",
+    "R22", "Q32", "R12", "C02", "Q22", "R40", "Q12", "C32", "P02", "C22", "C12", "P32",
+    "S90", "P22", "Y02", "P12", "Y32", "E02", "Q50", "Y22", "Q40", "E32", "R90", "Y12",
+    "E22", "S03", "Q60", "E12", "S33", "R03", "S23", "R33", "R23", "Q33", "Q70", "Q23",
+    "S13", "Q03", "C33", "R13", "C23", "P33", "Q13", "C03", "P23", "C13", "W00", "Y33",
+    "Q90", "Y23", "P13", "P03", "E33", "Q80", "E23", "G00", "Y03", "Y13", "W10", "T00",
     "H00", "E13", "E03",
 )
-VMEM_LIMIT = 52428800
+VMEM_LIMIT = 67043328
 
 
 def scoped(stage):
@@ -91,10 +86,11 @@
 def window(
     n_section,
     gain, arr, ret, wv_in, wo_in, saved_in, fresh_in, tgt_in, fill, read,
+    act_out, cot_out, stash_out, gv_out, go_out, gg_out,
     act, cot, stash, gv, go, gg,
     wv, wo, saved, fresh, tgt,
     nrm, cotf, nsv, xin, part, rsh, rsy, zq, keep, zs, zr, ysnd, dsnd, shf, shb, dgs, gacc, gsum,
-    in_s, ag_s, ag_r, rs_s, rs_r, sh_s, sh_r, g_s, g_r,
+    in_s, out_s, ag_s, ag_r, rs_s, rs_r, sh_s, sh_r, g_s, g_r,
 ):
     ticks = fresh.shape[0]
     slots = saved.shape[0]
@@ -102,6 +98,7 @@
     half = depth // 2
     rows = arr.shape[1]
     tokens = rows * YN * ZN
+    scale = (tokens * ticks) ** (-0.5)
     me = lax.axis_index("dp")
     sec = lax.axis_index("section")
     z, y = me // YN, me % YN
@@ -148,6 +145,13 @@
                 loads[name].wait()
                 loaded.add(name)
 
+    results = []
+
+    def put(src, dst):
+        copy = pltpu.make_async_copy(src, dst, out_s.at[len(results)])
+        results.append(copy)
+        copy.start()
+
     def send(src, dst, s, r, target):
         return pltpu.make_async_remote_copy(
             src_ref=src, dst_ref=dst, send_sem=s, recv_sem=r, device_id=target, device_id_type=MESH
@@ -158,8 +162,11 @@
 
     init_items = [(sl, g) for g in range(2) for sl in range(slots)]
 
-    def mode_of(row):
-        return STREAM_MODES[row][0] if row < 4 else INIT_MODE
+    def mode_of(row, t):
+        return STREAM_GATHERS[row][t] if row < 4 else INIT_GATHERS[row - 4]
+
+    def over_y(st, t):
+        return STREAM_SUMS[st][t] == "Y"
 
     def buf_of(row, t):
         if row >= 4:
@@ -171,49 +178,49 @@
         if arriving:
             dz, dy = (1 - dz, dy) if where == "z" else (dz, dy - where)
         block = buf_of(row, t).at[other(dz, dy), :, columns(h)]
-        i = [k for _, sends in GATHERS[mode_of(row)].values() for k in sends].index(key)
+        i = KEYS.index(key)
         return send(block, block, ag_s.at[row, i], ag_r.at[row, i], to(where))
 
     def gather(stage, row, t):
-        waits, sends = GATHERS[mode_of(row)][stage]
+        waits, sends = GATHERS[mode_of(row, t)][stage]
         for key in waits:
             gather_copy(row, t, key, arriving=True).wait_recv()
         for key in sends:
             gather_copy(row, t, key).start()
 
     def gather_drain(row, t):
-        for _, sends in GATHERS[mode_of(row)].values():
+        for _, sends in GATHERS[mode_of(row, t)].values():
             for key in sends:
                 gather_copy(row, t, key).wait_send()
 
-    def sum_copy(st, key):
+    def sum_copy(st, t, key):
         i = ("h1", "h3", "p1", "p3", "q").index(key)
-        over_y = STREAM_MODES[st][1] == "yr"
+        n = ZN if over_y(st, t) else 1
         if key == "q":
-            src, dst = (zs.at[st], zr.at[st]) if over_y else (part.at[st, zp], zq.at[st])
+            src, dst = (zs.at[st], zr.at[st]) if over_y(st, t) else (part.at[st, zp], zq.at[st])
             return send(src, dst, rs_s.at[st, i], rs_r.at[st, i], to("z"))
-        zz = pl.ds(0, ZN) if over_y else pl.ds(z, 1)
+        zz = pl.ds(0 if over_y(st, t) else z, n)
         way = 1 if key[1] == "1" else -1
         side = 0 if way == 1 else 1
         if key[0] == "h":
             src = part.at[st, zz, y_at(2), :, columns(side)]
-            dst = rsh.at[st, side, pl.ds(0, ZN if over_y else 1)]
+            dst = rsh.at[st, side, pl.ds(0, n)]
         else:
             src = part.at[st, zz, y_at(way)]
-            dst = rsy.at[st, side, pl.ds(0, ZN if over_y else 1)]
+            dst = rsy.at[st, side, pl.ds(0, n)]
         return send(src, dst, rs_s.at[st, i], rs_r.at[st, i], to(way))
 
-    def sum_wait(st, *keys):
+    def sum_wait(st, t, *keys):
         for key in keys:
-            sum_copy(st, key).wait_recv()
-
-    def sum_start(st, *keys):
+            sum_copy(st, t, key).wait_recv()
+
+    def sum_start(st, t, *keys):
         for key in keys:
-            sum_copy(st, key).start()
-
-    def sum_drain(st):
+            sum_copy(st, t, key).start()
+
+    def sum_drain(st, t):
         for key in ("h1", "h3", "p1", "p3", "q"):
-            sum_copy(st, key).wait_send()
+            sum_copy(st, t, key).wait_send()
 
     def add_halves(st, zz, slot):
         for side, way in ((0, 1), (1, -1)):
@@ -289,22 +296,22 @@
             dgs[g, t * tokens : (t + 1) * tokens, :] = down
             terms = dot_nt(down, wv[g])
         if t > 0:
-            sum_drain(st)
+            sum_drain(st, t - 1)
         part[st] = terms.reshape(ZN, YN, rows, depth).astype(BF16)
-        if STREAM_MODES[st][1] == "yr":
-            sum_start(st, "h1", "h3")
-        else:
-            sum_start(st, "q")
+        if over_y(st, t):
+            sum_start(st, t, "h1", "h3")
+        else:
+            sum_start(st, t, "q")
 
     @scoped
     def stage_p(st, t):
-        if STREAM_MODES[st][1] == "yr":
-            sum_wait(st, "h1", "h3")
+        if over_y(st, t):
+            sum_wait(st, t, "h1", "h3")
             for zz in range(ZN):
                 add_halves(st, zz, zz)
-            sum_start(st, "p1", "p3")
-        else:
-            sum_wait(st, "q")
+            sum_start(st, t, "p1", "p3")
+        else:
+            sum_wait(st, t, "q")
             for k in (2, 1, 3, 0):
                 both = part[st, z, y_at(k)].astype(F32) + zq[st, y_at(k)].astype(F32)
                 if k:
@@ -312,24 +319,24 @@
                 else:
                     keep[st] = both
                 if k == 2:
-                    sum_start(st, "h1", "h3")
+                    sum_start(st, t, "h1", "h3")
 
     @scoped
     def stage_y(st, t):
-        if STREAM_MODES[st][1] == "yr":
-            sum_wait(st, "p1", "p3")
+        if over_y(st, t):
+            sum_wait(st, t, "p1", "p3")
 
             def total(zz):
                 acc = part[st, zz, y].astype(F32) + rsy[st, 0, zz].astype(F32)
                 return acc + rsy[st, 1, zz].astype(F32)
 
             zs[st] = total(zp).astype(BF16)
-            sum_start(st, "q")
+            sum_start(st, t, "q")
             keep[st] = total(z)
         else:
-            sum_wait(st, "h1", "h3")
+            sum_wait(st, t, "h1", "h3")
             add_halves(st, z, 0)
-            sum_start(st, "p1", "p3")
+            sum_start(st, t, "p1", "p3")
 
     def pick(candidates, which):
         chosen = candidates[0][1]
@@ -339,17 +346,17 @@
 
     def source_rows(t, g):
         options = [(sl, saved[sl, g].astype(F32)) for sl in range(slots)]
-        options += [(fill[0, u, g], xin[u, g].astype(F32)) for u in range(t + 1)]
-        return pick(options, read[0, t, g])
+        options += [(fill[0, g, u], xin[u, g].astype(F32)) for u in range(t + 1)]
+        return pick(options, read[0, g, t])
 
     @scoped
     def stage_e(st, t):
         g = st % 2
-        if STREAM_MODES[st][1] == "yr":
-            sum_wait(st, "q")
+        if over_y(st, t):
+            sum_wait(st, t, "q")
             total = keep[st] + zr[st].astype(F32)
         else:
-            sum_wait(st, "p1", "p3")
+            sum_wait(st, t, "p1", "p3")
             total = keep[st] + rsy[st, 0, 0].astype(F32) + rsy[st, 1, 0].astype(F32)
         if st < B0:
             out = (xin[t, g].astype(F32) + total).astype(BF16)
@@ -368,8 +375,10 @@
             shift(st, t).start()
         elif st < B0:
             act[g] = out
+            put(act.at[g], act_out.at[g])
         else:
             cot[g] = out
+            put(cot.at[g], cot_out.at[g])
 
     @scoped
     def stage_w(g, _):
@@ -378,13 +387,15 @@
         picked = []
         for t in range(ticks):
             options = [(sl, nsv[sl, g].astype(F32)) for sl in range(slots)]
-            options += [(fill[0, u, g], nrm[2 * u + g].astype(F32)) for u in range(t + 1)]
-            picked.append(pick(options, read[0, t, g]).reshape(tokens, depth).astype(BF16))
+            options += [(fill[0, g, u], nrm[2 * u + g].astype(F32)) for u in range(t + 1)]
+            picked.append(pick(options, read[0, g, t]).reshape(tokens, depth).astype(BF16))
         normed = jnp.concatenate(picked, axis=0)
         values = dot_nn(normed, wv[g]).astype(BF16)
-        gv[g] = dot_tn(normed, dgs[g]).astype(BF16)
+        gv[g] = (dot_tn(normed, dgs[g]) * scale).astype(BF16)
+        put(gv.at[g], gv_out.at[g])
         upstream = jnp.concatenate([whole(cotf, 2 * t + g) for t in range(ticks)], axis=0)
-        go[g] = dot_tn(values, upstream).astype(BF16)
+        go[g] = (dot_tn(values, upstream) * scale).astype(BF16)
+        put(go.at[g], go_out.at[g])
 
     @scoped
     def stage_t(_, __):
@@ -392,8 +403,9 @@
             for g in range(2):
                 rows_now = saved[sl, g].astype(F32)
                 for t in range(ticks):
-                    rows_now = jnp.where(fill[0, t, g] == sl, xin[t, g].astype(F32), rows_now)
+                    rows_now = jnp.where(fill[0, g, t] == sl, xin[t, g].astype(F32), rows_now)
                 stash[sl, g] = rows_now.astype(BF16)
+        put(stash, stash_out)
 
     def gain_copy(i, arriving=False):
         peer = other(*others[i])
@@ -413,7 +425,8 @@
             j = others.index((dz, -dy % YN))
             peer = other(dz, dy)
             send(gsum.at[peer], gsum.at[peer], g_s.at[j], g_r.at[j], {"dp": peer}).wait_recv()
-        gg[...] = jnp.sum(gsum[...], axis=0) * (tokens * ticks) ** (-0.5)
+        gg[...] = jnp.sum(gsum[...], axis=0) * scale
+        put(gg, gg_out)
 
     pl.semaphore_wait(barrier, len(others) + 2)
     stages = {
@@ -424,13 +437,33 @@
         stages[step[0]](int(step[1]), int(step[2]))
     for st in range(4):
         gather_drain(st, ticks - 1)
-        sum_drain(st)
+        sum_drain(st, ticks - 1)
         for t in range(ticks - 1):
             shift(st, t).wait_send()
     for i in range(len(init_items)):
         gather_drain(4 + i, 0)
     for i in range(len(others)):
         gain_copy(i).wait_send()
+    for copy in results:
+        copy.wait()
+
+
+def finish(act, cot, stash, gv, go, gg, *refs):
+    n = 6
+    outs, held, sems = refs[:n], refs[n : 2 * n], refs[2 * n]
+    pieces = [
+        (src.at[i], dst.at[0, i], mid.at[i])
+        for src, dst, mid in zip((gv, go, stash, act, cot), (outs[3], outs[4], outs[2], outs[0], outs[1]), held)
+        for i in range(src.shape[0])
+    ]
+    pieces.append((gg, outs[5].at[0], held[5]))
+    for i, (src, _, mid) in enumerate(pieces):
+        pltpu.make_async_copy(src, mid, sems.at[0, i]).start()
+    for i, (src, dst, mid) in enumerate(pieces):
+        pltpu.make_async_copy(src, mid, sems.at[0, i]).wait()
+        pltpu.make_async_copy(mid, dst, sems.at[1, i]).start()
+    for i, (_, dst, mid) in enumerate(pieces):
+        pltpu.make_async_copy(mid, dst, sems.at[1, i]).wait()
 
 
 def body(n_section, *args):
@@ -444,24 +477,19 @@
     tokens = rows * YN * ZN
     vmem = pl.BlockSpec(memory_space=pltpu.VMEM)
     smem = pl.BlockSpec(memory_space=pltpu.SMEM)
-    hbm = pl.BlockSpec(memory_space=pltpu.HBM)
+    hbm = pl.BlockSpec(memory_space=pl.ANY)
     block = (rows, depth)
     n_rows = 4 + 2 * slots
     dma = pltpu.SemaphoreType.DMA
     held = [pltpu.VMEM(a.shape, a.dtype) for a in (wv, wo, saved, fresh, targets)]
+    results = [((2, *block), BF16)] * 2 + [((slots, 2, *block), BF16), (wv.shape, BF16), (wo.shape, BF16), ((2, depth), F32)]
     outs = pl.pallas_call(
         functools.partial(window, n_section),
-        out_shape=(
-            jax.ShapeDtypeStruct((2, *block), BF16),
-            jax.ShapeDtypeStruct((2, *block), BF16),
-            jax.ShapeDtypeStruct((slots, 2, *block), BF16),
-            jax.ShapeDtypeStruct(wv.shape, BF16),
-            jax.ShapeDtypeStruct(wo.shape, BF16),
-            jax.ShapeDtypeStruct((2, depth), F32),
-        ),
+        out_shape=[jax.ShapeDtypeStruct(*r) for r in results],
         in_specs=[vmem] * 3 + [hbm] * 5 + [smem] * 2,
-        out_specs=[vmem] * 6,
-        scratch_shapes=held
+        out_specs=[hbm] * 6,
+        scratch_shapes=[pltpu.VMEM(*r) for r in results]
+        + held
         + [
             pltpu.VMEM((2 * ticks, 8, *block), BF16),
             pltpu.VMEM((2 * ticks, 8, *block), BF16),
@@ -482,8 +510,9 @@
             pltpu.VMEM((2, *block), F32),
             pltpu.VMEM((8, 2, depth), F32),
             dma((len(held),)),
-            dma((n_rows, N_KEYS)),
-            dma((n_rows, N_KEYS)),
+            dma((10,)),
+            dma((n_rows, len(KEYS))),
+            dma((n_rows, len(KEYS))),
             dma((4, 5)),
             dma((4, 5)),
             dma((ticks - 1, 4)),
@@ -495,12 +524,16 @@
             collective_id=0, has_side_effects=True, vmem_limit_bytes=VMEM_LIMIT
         ),
         name="window",
-    )(gain, arr, ret, wv, wo, saved, fresh, targets, fill, read)
-    act, cot, stash, gv, go, gg = outs
-    scale = jnp.asarray((ticks * tokens) ** (-0.5), F32)
-    gv = (gv.astype(F32) * scale).astype(BF16)
-    go = (go.astype(F32) * scale).astype(BF16)
-    return tuple(a[None] for a in (act, cot, stash, gv, go, gg))
+    )(gain, arr, ret, wv, wo, saved, fresh, targets, fill.swapaxes(1, 2), read.swapaxes(1, 2))
+    return pl.pallas_call(
+        finish,
+        out_shape=[jax.ShapeDtypeStruct((1, *shape), dtype) for shape, dtype in results],
+        in_specs=[hbm] * 6,
+        out_specs=[hbm] * 6,
+        scratch_shapes=[pltpu.VMEM(*results[i]) for i in (3, 4, 2, 0, 1, 5)] + [dma((2, 12))],
+        compiler_params=pltpu.CompilerParams(vmem_limit_bytes=VMEM_LIMIT),
+        name="finish",
+    )(*outs)
 
 
 def solution(mesh):

time: 199 us -> 179 us (0.90)
  local copies, waits for them, and re-layouts: 9.75 us -> 0 us
  Pallas kernels: 182 us -> 176 us
  other arithmetic: 5.47 us -> 0 us
    unnamed x20 -> x0, local copies, waits for them, and re-layouts: 9.75 us -> none
    pallas_call x1 -> x2, Pallas kernels: 182 us -> 176 us  [the longest x1 172 us: body(): pl.pallas_call(functools.partial(window, n_section), out_shape=[jax.Shape...]
    broadcast_in_dim x2 -> x0, other arithmetic: 5.47 us -> none  [body(): return tuple((a[None] for a in (act, cot, stash, gv, go, gg)))]
where the time goes in v3:
time: 179 us; the launch traced here: 177 us
  Pallas kernels  176 us (98%)
    pallas_call x1, Pallas kernels, body(): pl.pallas_call(functools.partial(window, n_section), out_shape=[jax.Shape...  172 us
    pallas_call x1, Pallas kernels, body(): pl.pallas_call(finish, out_shape=[jax.ShapeDtypeStruct((1, *shape), dtype...  4.23 us

profile of v3, /device:TPU:32, one launch (start us, length us, event | category | flops | bytes accessed | tf_op | source)
XLA Modules:
  0.0 176.8 jit_solution(1859004842731156490)
XLA Ops:
  0.6 171.8 %window.1 = (bf16[2,8,4608]{2,1,0:T(8,128)(2,1)}, bf16[2,8,4608]{2,1,0:T(8,128)(2,1)}, bf16[3,2,8,4608]{3,2,1,0:T(8,128)(2,1)}, bf16[2,4608,128]{2,1,0:T(8,128)(...) custom-call(f32[2,4608]{1,0:T(2,128)} %bitcast.13, bf16[2,8,4608]{2,1,0:T(8,128)(2,1)} %bitcast.11, ...), custom_call_target="tpu_custom_call" | custom-call | tf_op jit(solution)/shard_map/window/pallas_call | solution.py:486
  172.4 4.2 %finish.1 = (bf16[1,2,8,4608]{3,2,1,0:T(8,128)(2,1)}, bf16[1,2,8,4608]{3,2,1,0:T(8,128)(2,1)}, bf16[1,3,2,8,4608]{4,3,2,1,0:T(8,128)(2,1)}, bf16[1,2,4608,128]{3...) custom-call(bf16[2,8,4608]{2,1,0:T(8,128)(2,1)} %get-tuple-element.12.act, ...), custom_call_target="tpu_custom_call" | custom-call | tf_op jit(solution)/shard_map/finish/pallas_call | solution.py:528

commit v4 on v3

--- a/solution.py
+++ b/solution.py
@@ -29,6 +29,11 @@
     "v3": ((1, 1, 1), -1),
 }
 KEYS = tuple(PIECES)
+SUM_SENDS = {
+    "Y": ("h1", "h3", "p1", "p3", "r1", "r3", "q2"),
+    "Z": ("q2", "q1", "q3", "q0", "h1", "h3", "p1", "p3"),
+}
+SUM_KEYS = ("h1", "h3", "p1", "p3", "r1", "r3", "q2", "q1", "q3", "q0")
 GATHERS = {
     "Y": {
         "S": ((), ("y1", "y3", "z0")),
@@ -43,22 +48,22 @@
         "C": (("h1", "h3", "v1", "v3"), ()),
     },
 }
-STREAM_GATHERS = ("YZZY", "ZYYY", "ZYZY", "YZYZ")
-STREAM_SUMS = ("YYYZ", "YYYY", "ZYZY", "YZYY")
-INIT_GATHERS = "ZYZZYZ"
+STREAM_GATHERS = ("YZYZ", "YYZZ", "ZZYZ", "ZZZY")
+STREAM_SUMS = ("YZYZ", "ZYYY", "YYZY", "YZYZ")
+INIT_GATHERS = "YZZYZY"
 ORDER = (
-    "S00", "S10", "S20", "R00", "S30", "R10", "R20", "Q00", "R30", "Q10", "Q20", "C00",
-    "S80", "Q30", "C10", "C20", "P00", "C30", "P10", "Y00", "P30", "P20", "S50", "E00",
-    "S60", "Y10", "Y30", "Y20", "S01", "E10", "E30", "S70", "E20", "S40", "R01", "S11",
-    "S31", "S21", "R11", "Q01", "R31", "Q11", "R21", "Q31", "C01", "Q21", "C11", "C31",
-    "P01", "C21", "P11", "Y01", "R50", "P31", "P21", "E01", "Y31", "R60", "Y11", "Y21",
-    "E31", "S02", "R70", "E21", "E11", "R80", "R02", "S32", "S22", "S12", "R32", "Q02",
-    "R22", "Q32", "R12", "C02", "Q22", "R40", "Q12", "C32", "P02", "C22", "C12", "P32",
-    "S90", "P22", "Y02", "P12", "Y32", "E02", "Q50", "Y22", "Q40", "E32", "R90", "Y12",
-    "E22", "S03", "Q60", "E12", "S33", "R03", "S23", "R33", "R23", "Q33", "Q70", "Q23",
-    "S13", "Q03", "C33", "R13", "C23", "P33", "Q13", "C03", "P23", "C13", "W00", "Y33",
-    "Q90", "Y23", "P13", "P03", "E33", "Q80", "E23", "G00", "Y03", "Y13", "W10", "T00",
-    "H00", "E13", "E03",
+    "S00", "S30", "S20", "R00", "S10", "R30", "Q00", "R10", "R20", "Q30", "Q10", "S40",
+    "C00", "Q20", "C30", "C10", "P00", "C20", "P10", "Y00", "P30", "Y10", "S80", "Y30",
+    "E00", "P20", "E10", "E30", "S60", "Y20", "S01", "S11", "E20", "S31", "R01", "R11",
+    "Q01", "S21", "R31", "Q11", "C01", "R21", "Q31", "C11", "Q21", "P01", "S50", "C31",
+    "P11", "P31", "Y01", "Y11", "C21", "S70", "E01", "Y31", "E11", "P21", "R40", "R50",
+    "E31", "Y21", "S02", "S12", "E21", "S32", "R02", "Q50", "R12", "Q40", "Q02", "S22",
+    "R32", "R22", "Q12", "Q32", "C02", "Q22", "R70", "C12", "C32", "P02", "C22", "P32",
+    "P22", "Y02", "P12", "Y32", "Y22", "E02", "R60", "Y12", "R80", "E32", "E22", "S90",
+    "E12", "S03", "S33", "S23", "S13", "R33", "R23", "R03", "Q33", "Q23", "R90", "R13",
+    "C33", "Q60", "Q03", "Q13", "Q80", "C23", "P33", "C03", "C13", "P23", "Y33", "W00",
+    "P03", "Y23", "T00", "P13", "Q70", "E33", "Q90", "E23", "G00", "Y03", "Y13", "W10",
+    "E03", "H00", "E13",
 )
 VMEM_LIMIT = 67043328
 
@@ -85,11 +90,11 @@
 
 def window(
     n_section,
-    gain, arr, ret, wv_in, wo_in, saved_in, fresh_in, tgt_in, fill, read,
+    gain_in, arr_in, ret_in, wv_in, wo_in, saved_in, fresh_in, tgt_in, fill, read,
     act_out, cot_out, stash_out, gv_out, go_out, gg_out,
     act, cot, stash, gv, go, gg,
-    wv, wo, saved, fresh, tgt,
-    nrm, cotf, nsv, xin, part, rsh, rsy, zq, keep, zs, zr, ysnd, dsnd, shf, shb, dgs, gacc, gsum,
+    gain, arr, ret, wv, wo, saved, fresh, tgt,
+    nrm, cotf, nsv, xin, part, rsh, rsy, zq, zs, zr, ysnd, dsnd, shf, shb, dgs, gacc, gsum,
     in_s, out_s, ag_s, ag_r, rs_s, rs_r, sh_s, sh_r, g_s, g_r,
 ):
     ticks = fresh.shape[0]
@@ -126,6 +131,9 @@
         pl.semaphore_signal(barrier, inc=1, device_id=target, device_id_type=MESH)
 
     loads = {
+        "arr": (arr_in, arr),
+        "gain": (gain_in, gain),
+        "ret": (ret_in, ret),
         "wv": (wv_in, wv),
         "wo": (wo_in, wo),
         "saved": (saved_in, saved),
@@ -194,21 +202,22 @@
                 gather_copy(row, t, key).wait_send()
 
     def sum_copy(st, t, key):
-        i = ("h1", "h3", "p1", "p3", "q").index(key)
-        n = ZN if over_y(st, t) else 1
-        if key == "q":
-            src, dst = (zs.at[st], zr.at[st]) if over_y(st, t) else (part.at[st, zp], zq.at[st])
-            return send(src, dst, rs_s.at[st, i], rs_r.at[st, i], to("z"))
-        zz = pl.ds(0 if over_y(st, t) else z, n)
+        i = SUM_KEYS.index(key)
+        sems = (rs_s.at[st, i], rs_r.at[st, i])
+        if key[0] == "q":
+            if over_y(st, t):
+                return send(zs.at[st], zr.at[st], *sems, to("z"))
+            k = y_at(int(key[1]))
+            return send(part.at[st, zp, k], zq.at[st, k], *sems, to("z"))
         way = 1 if key[1] == "1" else -1
         side = 0 if way == 1 else 1
         if key[0] == "h":
-            src = part.at[st, zz, y_at(2), :, columns(side)]
-            dst = rsh.at[st, side, pl.ds(0, n)]
-        else:
-            src = part.at[st, zz, y_at(way)]
-            dst = rsy.at[st, side, pl.ds(0, n)]
-        return send(src, dst, rs_s.at[st, i], rs_r.at[st, i], to(way))
+            n = ZN if over_y(st, t) else 1
+            src = part.at[st, pl.ds(0 if over_y(st, t) else z, n), y_at(2), :, columns(side)]
+            return send(src, rsh.at[st, side, pl.ds(0, n)], *sems, to(way))
+        zz = zp if over_y(st, t) and key[0] == "p" else z
+        at = zz if over_y(st, t) else 0
+        return send(part.at[st, zz, y_at(way)], rsy.at[st, side, at], *sems, to(way))
 
     def sum_wait(st, t, *keys):
         for key in keys:
@@ -219,7 +228,7 @@
             sum_copy(st, t, key).start()
 
     def sum_drain(st, t):
-        for key in ("h1", "h3", "p1", "p3", "q"):
+        for key in SUM_SENDS[STREAM_SUMS[st][t]]:
             sum_copy(st, t, key).wait_send()
 
     def add_halves(st, zz, slot):
@@ -244,7 +253,7 @@
     @scoped
     def stage_s(st, t):
         if st >= 4:
-            need("saved")
+            need("saved", "gain")
             sl, g = init_items[st - 4]
             buf_of(st, t)[me] = normed_of(saved[sl, g].astype(F32), g)[2]
             gather("S", st, t)
@@ -253,7 +262,9 @@
         if t > 0:
             shift(st, t - 1).wait_recv()
         if st < B0:
+            need("gain")
             if t == 0:
+                need("arr")
                 x = arr[g].astype(F32)
             else:
                 need("fresh")
@@ -262,6 +273,7 @@
             xin[t, g] = x.astype(BF16)
             own = normed_of(x, g)[2]
         elif t == 0:
+            need("ret")
             own = ret[g]
         else:
             if g == 0:
@@ -301,42 +313,42 @@
         if over_y(st, t):
             sum_start(st, t, "h1", "h3")
         else:
-            sum_start(st, t, "q")
+            sum_start(st, t, "q2", "q1", "q3", "q0")
 
     @scoped
     def stage_p(st, t):
         if over_y(st, t):
             sum_wait(st, t, "h1", "h3")
-            for zz in range(ZN):
-                add_halves(st, zz, zz)
+            add_halves(st, zp, zp)
             sum_start(st, t, "p1", "p3")
-        else:
-            sum_wait(st, t, "q")
-            for k in (2, 1, 3, 0):
-                both = part[st, z, y_at(k)].astype(F32) + zq[st, y_at(k)].astype(F32)
-                if k:
-                    part[st, z, y_at(k)] = both.astype(BF16)
-                else:
-                    keep[st] = both
-                if k == 2:
-                    sum_start(st, t, "h1", "h3")
+            add_halves(st, z, z)
+            sum_start(st, t, "r1", "r3")
+        else:
+            sum_wait(st, t, "q2")
+            add_block(st, 2)
+            sum_start(st, t, "h1", "h3")
 
     @scoped
     def stage_y(st, t):
         if over_y(st, t):
             sum_wait(st, t, "p1", "p3")
-
-            def total(zz):
-                acc = part[st, zz, y].astype(F32) + rsy[st, 0, zz].astype(F32)
-                return acc + rsy[st, 1, zz].astype(F32)
-
-            zs[st] = total(zp).astype(BF16)
-            sum_start(st, t, "q")
-            keep[st] = total(z)
-        else:
+            zs[st] = total_at(st, zp, zp).astype(BF16)
+            sum_start(st, t, "q2")
+        else:
+            sum_wait(st, t, "q1", "q3")
+            add_block(st, 1)
+            add_block(st, 3)
             sum_wait(st, t, "h1", "h3")
             add_halves(st, z, 0)
             sum_start(st, t, "p1", "p3")
+
+    def add_block(st, k):
+        at = (st, z, y_at(k))
+        part[at] = (part[at].astype(F32) + zq[st, y_at(k)].astype(F32)).astype(BF16)
+
+    def total_at(st, zz, slot):
+        acc = part[st, zz, y].astype(F32) + rsy[st, 0, slot].astype(F32)
+        return acc + rsy[st, 1, slot].astype(F32)
 
     def pick(candidates, which):
         chosen = candidates[0][1]
@@ -353,11 +365,11 @@
     def stage_e(st, t):
         g = st % 2
         if over_y(st, t):
-            sum_wait(st, t, "q")
-            total = keep[st] + zr[st].astype(F32)
-        else:
-            sum_wait(st, t, "p1", "p3")
-            total = keep[st] + rsy[st, 0, 0].astype(F32) + rsy[st, 1, 0].astype(F32)
+            sum_wait(st, t, "r1", "r3", "q2")
+            total = total_at(st, z, z) + zr[st].astype(F32)
+        else:
+            sum_wait(st, t, "q0", "p1", "p3")
+            total = total_at(st, z, 0) + zq[st, y].astype(F32)
         if st < B0:
             out = (xin[t, g].astype(F32) + total).astype(BF16)
             ysnd[t, g] = out
@@ -371,6 +383,10 @@
             dsnd[t, g] = out
             term = total * scaled
             gacc[g] = term if t == 0 else gacc[g] + term
+        if t > 0:
+            shift(st, t - 1).wait_send()
+        if t == ticks - 1:
+            gather_drain(st, t)
         if t < ticks - 1:
             shift(st, t).start()
         elif st < B0:
@@ -384,6 +400,7 @@
     def stage_w(g, _):
         for i in range(slots):
             gather("C", 4 + g * slots + i, 0)
+            gather_drain(4 + g * slots + i, 0)
         picked = []
         for t in range(ticks):
             options = [(sl, nsv[sl, g].astype(F32)) for sl in range(slots)]
@@ -428,6 +445,7 @@
         gg[...] = jnp.sum(gsum[...], axis=0) * scale
         put(gg, gg_out)
 
+    need("arr", "gain", "ret")
     pl.semaphore_wait(barrier, len(others) + 2)
     stages = {
         "S": stage_s, "R": stage_r, "Q": stage_q, "C": stage_c, "P": stage_p, "Y": stage_y,
@@ -436,12 +454,7 @@
     for step in ORDER:
         stages[step[0]](int(step[1]), int(step[2]))
     for st in range(4):
-        gather_drain(st, ticks - 1)
         sum_drain(st, ticks - 1)
-        for t in range(ticks - 1):
-            shift(st, t).wait_send()
-    for i in range(len(init_items)):
-        gather_drain(4 + i, 0)
     for i in range(len(others)):
         gain_copy(i).wait_send()
     for copy in results:
@@ -475,18 +488,17 @@
     slots = saved.shape[0]
     feats = wv.shape[2]
     tokens = rows * YN * ZN
-    vmem = pl.BlockSpec(memory_space=pltpu.VMEM)
     smem = pl.BlockSpec(memory_space=pltpu.SMEM)
     hbm = pl.BlockSpec(memory_space=pl.ANY)
     block = (rows, depth)
     n_rows = 4 + 2 * slots
     dma = pltpu.SemaphoreType.DMA
-    held = [pltpu.VMEM(a.shape, a.dtype) for a in (wv, wo, saved, fresh, targets)]
+    held = [pltpu.VMEM(a.shape, a.dtype) for a in (gain, arr, ret, wv, wo, saved, fresh, targets)]
     results = [((2, *block), BF16)] * 2 + [((slots, 2, *block), BF16), (wv.shape, BF16), (wo.shape, BF16), ((2, depth), F32)]
     outs = pl.pallas_call(
         functools.partial(window, n_section),
         out_shape=[jax.ShapeDtypeStruct(*r) for r in results],
-        in_specs=[vmem] * 3 + [hbm] * 5 + [smem] * 2,
+        in_specs=[hbm] * 8 + [smem] * 2,
         out_specs=[hbm] * 6,
         scratch_shapes=[pltpu.VMEM(*r) for r in results]
         + held
@@ -499,7 +511,6 @@
             pltpu.VMEM((4, 2, ZN, rows, depth // 2), BF16),
             pltpu.VMEM((4, 2, ZN, *block), BF16),
             pltpu.VMEM((4, YN, *block), BF16),
-            pltpu.VMEM((4, *block), F32),
             pltpu.VMEM((4, *block), BF16),
             pltpu.VMEM((4, *block), BF16),
             pltpu.VMEM((ticks, 2, *block), BF16),
@@ -513,8 +524,8 @@
             dma((10,)),
             dma((n_rows, len(KEYS))),
             dma((n_rows, len(KEYS))),
-            dma((4, 5)),
-            dma((4, 5)),
+            dma((4, len(SUM_KEYS))),
+            dma((4, len(SUM_KEYS))),
             dma((ticks - 1, 4)),
             dma((ticks - 1, 4)),
             dma((7,)),

time: 179 us -> 174 us (0.972)
  Pallas kernels: 176 us -> 173 us
    pallas_call x1, Pallas kernels: 172 us -> 168 us  [body(): pl.pallas_call(functools.partial(window, n_section), out_shape=[jax.Shape...]
where the time goes in v4:
time: 174 us; the launch traced here: 173 us
  Pallas kernels  173 us (99%)
    pallas_call x1, Pallas kernels, body(): pl.pallas_call(functools.partial(window, n_section), out_shape=[jax.Shape...  168 us
    pallas_call x1, Pallas kernels, body(): pl.pallas_call(finish, out_shape=[jax.ShapeDtypeStruct((1, *shape), dtype...  4.23 us

profile of v4, /device:TPU:32, one launch (start us, length us, event | category | flops | bytes accessed | tf_op | source)
XLA Modules:
  0.0 173.5 jit_solution(1994485598204194898)
XLA Ops:
  0.6 168.5 %window.1 = (bf16[2,8,4608]{2,1,0:T(8,128)(2,1)}, bf16[2,8,4608]{2,1,0:T(8,128)(2,1)}, bf16[3,2,8,4608]{3,2,1,0:T(8,128)(2,1)}, bf16[2,4608,128]{2,1,0:T(8,128)(...) custom-call(f32[2,4608]{1,0:T(2,128)} %bitcast.13, bf16[2,8,4608]{2,1,0:T(8,128)(2,1)} %bitcast.11, ...), custom_call_target="tpu_custom_call" | custom-call | tf_op jit(solution)/shard_map/window/pallas_call | solution.py:498
  169.1 4.2 %finish.1 = (bf16[1,2,8,4608]{3,2,1,0:T(8,128)(2,1)}, bf16[1,2,8,4608]{3,2,1,0:T(8,128)(2,1)}, bf16[1,3,2,8,4608]{4,3,2,1,0:T(8,128)(2,1)}, bf16[1,2,4608,128]{3...) custom-call(bf16[2,8,4608]{2,1,0:T(8,128)(2,1)} %get-tuple-element.12.act, ...), custom_call_target="tpu_custom_call" | custom-call | tf_op jit(solution)/shard_map/finish/pallas_call | solution.py:539

commit v5 on v4

--- a/solution.py
+++ b/solution.py
@@ -431,8 +431,8 @@
 
     @scoped
     def stage_g(_, __):
-        for g in range(2):
-            gsum[me, g : g + 1, :] = jnp.sum(gacc[g], axis=0, keepdims=True)
+        sums = [jnp.sum(gacc[g], axis=0, keepdims=True) for g in range(2)]
+        gsum[me] = jnp.concatenate(sums, axis=0).astype(BF16)
         for i in range(len(others)):
             gain_copy(i).start()
 
@@ -442,7 +442,7 @@
             j = others.index((dz, -dy % YN))
             peer = other(dz, dy)
             send(gsum.at[peer], gsum.at[peer], g_s.at[j], g_r.at[j], {"dp": peer}).wait_recv()
-        gg[...] = jnp.sum(gsum[...], axis=0) * scale
+        gg[...] = jnp.sum(gsum[...].astype(F32), axis=0) * scale
         put(gg, gg_out)
 
     need("arr", "gain", "ret")
@@ -464,11 +464,13 @@
 def finish(act, cot, stash, gv, go, gg, *refs):
     n = 6
     outs, held, sems = refs[:n], refs[n : 2 * n], refs[2 * n]
-    pieces = [
-        (src.at[i], dst.at[0, i], mid.at[i])
-        for src, dst, mid in zip((gv, go, stash, act, cot), (outs[3], outs[4], outs[2], outs[0], outs[1]), held)
-        for i in range(src.shape[0])
-    ]
+    pieces = []
+    for src, dst, mid, cuts in zip((gv, go, stash, act, cot), (outs[3], outs[4], outs[2], outs[0], outs[1]), held, (4, 4, 1, 1, 1)):
+        for i in range(src.shape[0]):
+            n_rows = src.shape[1] // cuts
+            for c in range(cuts):
+                part = pl.ds(c * n_rows, n_rows)
+                pieces.append((src.at[i, part], dst.at[0, i, part], mid.at[i, part]))
     pieces.append((gg, outs[5].at[0], held[5]))
     for i, (src, _, mid) in enumerate(pieces):
         pltpu.make_async_copy(src, mid, sems.at[0, i]).start()
@@ -519,7 +521,7 @@
             pltpu.VMEM((ticks - 1, 2, *block), BF16),
             pltpu.VMEM((2, ticks * tokens, feats), BF16),
             pltpu.VMEM((2, *block), F32),
-            pltpu.VMEM((8, 2, depth), F32),
+            pltpu.VMEM((8, 2, depth), BF16),
             dma((len(held),)),
             dma((10,)),
             dma((n_rows, len(KEYS))),
@@ -541,7 +543,7 @@
         out_shape=[jax.ShapeDtypeStruct((1, *shape), dtype) for shape, dtype in results],
         in_specs=[hbm] * 6,
         out_specs=[hbm] * 6,
-        scratch_shapes=[pltpu.VMEM(*results[i]) for i in (3, 4, 2, 0, 1, 5)] + [dma((2, 12))],
+        scratch_shapes=[pltpu.VMEM(*results[i]) for i in (3, 4, 2, 0, 1, 5)] + [dma((2, 24))],
         compiler_params=pltpu.CompilerParams(vmem_limit_bytes=VMEM_LIMIT),
         name="finish",
     )(*outs)

time: 174 us -> 174 us (level)
  no operation moved by 1% of the time
where the time goes in v5:
time: 174 us
  Pallas kernels  173 us (99%)
    pallas_call x1, Pallas kernels, body(): pl.pallas_call(functools.partial(window, n_section), out_shape=[jax.Shape...  168 us
    pallas_call x1, Pallas kernels, body(): pl.pallas_call(finish, out_shape=[jax.ShapeDtypeStruct((1, *shape), dtype...  5.13 us

profile of v5, /device:TPU:32, one launch (start us, length us, event | category | flops | bytes accessed | tf_op | source)
XLA Modules:
  0.0 173.6 jit_solution(1065435203890619689)
XLA Ops:
  0.6 167.7 %window.1 = (bf16[2,8,4608]{2,1,0:T(8,128)(2,1)}, bf16[2,8,4608]{2,1,0:T(8,128)(2,1)}, bf16[3,2,8,4608]{3,2,1,0:T(8,128)(2,1)}, bf16[2,4608,128]{2,1,0:T(8,128)(...) custom-call(f32[2,4608]{1,0:T(2,128)} %bitcast.13, bf16[2,8,4608]{2,1,0:T(8,128)(2,1)} %bitcast.11, ...), custom_call_target="tpu_custom_call" | custom-call | tf_op jit(solution)/shard_map/window/pallas_call | solution.py:500
  168.3 5.1 %finish.1 = (bf16[1,2,8,4608]{3,2,1,0:T(8,128)(2,1)}, bf16[1,2,8,4608]{3,2,1,0:T(8,128)(2,1)}, bf16[1,3,2,8,4608]{4,3,2,1,0:T(8,128)(2,1)}, bf16[1,2,4608,128]{3...) custom-call(bf16[2,8,4608]{2,1,0:T(8,128)(2,1)} %get-tuple-element.12.act, ...), custom_call_target="tpu_custom_call" | custom-call | tf_op jit(solution)/shard_map/finish/pallas_call | solution.py:541
